TPU v7x, 128 devices: a whole 4x4x4 slice. The times are simulated.
128 devices in a mesh: tp: 2 (over core), dp: 64 (over z, y, x).
Axes of the slice: x: 4, y: 4, z: 4, core: 2. Of those that a mesh axis runs over, the one named last changes fastest.
Arguments:
- x_saved: bfloat16 [64, 2048, 1024], P('dp', 'tp')
- dy_out: bfloat16 [64, 2048, 1024], P('dp', 'tp')
- ln_params: float32 [4, 1024], replicated
- w_qkv: bfloat16 [1024, 16, 3, 64], P(None, 'tp')
- w_out: bfloat16 [1024, 1024], P('tp')
- w_up: bfloat16 [1024, 4096], P(None, 'tp')
- w_down: bfloat16 [4096, 1024], P('tp')
Outputs:
- output 1: bfloat16 [64, 2048, 1024], P('dp', 'tp')
- output 2: float32 [4, 1024], replicated
- output 3: float32 [1024, 16, 3, 64], P('dp', 'tp')
- output 4: float32 [1024, 1024], P(('tp', 'dp'))
- output 5: float32 [1024, 4096], P('dp', 'tp')
- output 6: float32 [4096, 1024], P(('tp', 'dp'))
All inputs are finite; a program needn't handle non-finite values.
Results may differ from a plain program's by a relative error of at most 0.00983313.
Values are sent between devices in bfloat16 or wider.
A program may use at most 1 GiB of HBM per device.

v0:
```python
import math

import jax
import jax.numpy as jnp
import numpy as np
from jax import lax
from jax.experimental import pallas as pl
from jax.experimental.pallas import tpu as pltpu
from jax.sharding import PartitionSpec as P

NORM_EPS = 1e-5
ROPE_BASE = 10000.0
F32, BF16 = jnp.float32, jnp.bfloat16
LOG2E = math.log2(math.e)
T = 2048
HALF = T // 2
TILE = 256
SMALL = 128
TT = 512
FC = 1024
LANES = 128
VMEM_LIMIT = 63 << 20
AXES = ('z', 'y', 'x')
AXIS_STRIDE = {'z': 16, 'y': 4, 'x': 1}
RING = 4


def dot(a, b):
    return jnp.dot(a, b, preferred_element_type=F32)


def dot_nt(a, b):
    return lax.dot_general(a, b, (((1,), (1,)), ((), ())), preferred_element_type=F32)


def rope_tables():
    inv_freq = ROPE_BASE ** (-2.0 * jnp.arange(32, dtype=F32) / 64)
    angles = inv_freq[:, None] * jnp.arange(T, dtype=F32)[None, :]
    return jnp.cos(angles), jnp.sin(angles)


def ring_place(axis):
    return lax.rem(lax.div(lax.axis_index('dp'), AXIS_STRIDE[axis]), RING)


def ring_chip(axis, ahead):
    place = ring_place(axis)
    return {'dp': lax.axis_index('dp') + (lax.rem(place + ahead, RING) - place) * AXIS_STRIDE[axis]}


def other_core():
    return {'tp': 1 - lax.axis_index('tp')}


def send_to(device, src, dst, send_sem, recv_sem):
    return pltpu.make_async_remote_copy(src_ref=src, dst_ref=dst, send_sem=send_sem, recv_sem=recv_sem,
                                        device_id=device, device_id_type=pl.DeviceIdType.MESH)


def greet(devices):
    barrier = pltpu.get_barrier_semaphore()
    for device in devices:
        pl.semaphore_signal(barrier, inc=1, device_id=device, device_id_type=pl.DeviceIdType.MESH)
    pl.semaphore_wait(barrier, len(devices))


class TorusSum:
    COUNT = 30

    @staticmethod
    def half_shape(rows, width, by_cols):
        return (rows, width // 2) if by_cols else (rows // 2, width)

    @staticmethod
    def scratch(rows, width, by_cols=False):
        half, whole = TorusSum.half_shape(rows, width, by_cols), (rows, width)
        shapes = []
        for lead in ((RING, RING), (RING,), ()):
            shapes += [pltpu.VMEM(lead + half, F32)] * 8 + [pltpu.VMEM(lead + whole, F32)]
        return shapes + [pltpu.SemaphoreType.DMA((18,)), pltpu.SemaphoreType.DMA((18,)), pltpu.SemaphoreType.DMA((3,))]

    def __init__(self, grad, order, rows, col, width, refs, by_cols=False, in_vmem=False):
        self.grad, self.order, self.col, self.by_cols, self.in_vmem = grad, order, col, by_cols, in_vmem
        self.whole, self.half = (rows, width), TorusSum.half_shape(rows, width, by_cols)
        self.cols = pl.ds(col, width)
        self.refs, (self.send, self.recv, self.load) = refs, refs[27:]
        self.kept = [[axis for axis in AXES if axis not in order[:n]] for n in range(3)]

    def bufs(self, phase):
        return self.refs[9 * phase:9 * phase + 9]

    def part(self, which, col=0):
        shape = self.whole if which == 2 else self.half
        start = [0, col]
        if which == 1:
            start[self.by_cols] += self.half[self.by_cols]
        return tuple(pl.ds(first, size) for first, size in zip(start, shape))

    def block(self, phase, ahead, which):
        index = lax.rem(ring_place(self.order[phase]) + ahead, RING)
        lead = tuple(index if axis == self.order[phase] else slice(None) for axis in self.kept[phase])
        if phase == 0:
            return self.grad.at[lead + self.part(which, self.col)]
        return self.refs[9 * phase - 1].at[lead + self.part(which)]

    def load_copy(self, n):
        ahead, which = ((1, 0), (3, 1), (0, 2))[n]
        return pltpu.make_async_copy(self.block(0, ahead, which), self.bufs(0)[6 + n], self.load.at[n])

    def copy(self, phase, n):
        bufs = self.bufs(phase)
        src = bufs[2 + n] if n >= 4 else self.block(phase, *((2, 0), (1, 1), (2, 1), (3, 0))[n])
        chip = ring_chip(self.order[phase], (1, 1, 3, 3, 1, 3)[n])
        return send_to(chip, src, bufs[n], self.send.at[6 * phase + n], self.recv.at[6 * phase + n])

    def loads(self, phase):
        return phase == 0 and not self.in_vmem

    def start(self, phase):
        for n in (0, 2, 1, 3):
            self.copy(phase, n).start()
        if self.loads(phase):
            for n in range(3):
                self.load_copy(n).start()

    def add(self, phase):
        bufs = self.bufs(phase)
        own = self.block(phase, 1, 0), self.block(phase, 3, 1)
        if self.loads(phase):
            own = bufs[6], bufs[7]
            self.load_copy(0).wait()
            self.load_copy(1).wait()
        self.copy(phase, 0).wait_recv()
        self.copy(phase, 2).wait_recv()

        def rows(at):
            bufs[6][at] = own[0][at] + bufs[0][at]
            bufs[7][at] = own[1][at] + bufs[2][at]
        self.each(phase, rows)

    def each(self, phase, body):
        if phase == 0:
            def step(n, carry):
                body(n)
                return carry
            lax.fori_loop(0, RING, step, 0)
        else:
            body(slice(None))

    def pass_on(self, phase):
        self.copy(phase, 4).start()
        self.copy(phase, 5).start()

    def finish(self, phase):
        bufs = self.bufs(phase)
        lead = (slice(None),) * (2 - phase)
        low, high = bufs[8].at[lead + self.part(0)], bufs[8].at[lead + self.part(1)]
        own = self.block(phase, 0, 0), self.block(phase, 0, 1)
        if self.loads(phase):
            own = low, high
            self.load_copy(2).wait()
        for n in (1, 3, 4, 5):
            self.copy(phase, n).wait_recv()

        def rows(at):
            low[at] = own[0][at] + bufs[3][at] + bufs[4][at]
            high[at] = own[1][at] + bufs[1][at] + bufs[5][at]
        self.each(phase, rows)

    def drain(self):
        for phase in range(3):
            for n in range(6):
                self.copy(phase, n).wait_send()

    @property
    def result(self):
        return self.refs[26]


def plan_columns(rows, tiles, by_cols=False):
    plan, col = [], 0
    for order, count in zip((('x', 'y', 'z'), ('y', 'z', 'x'), ('z', 'x', 'y')), tiles):
        plan.append((order, rows, col, count * LANES, by_cols))
        col += count * LANES
    return plan


def plan_scratch(plans):
    return [shape for plan in plans for _, rows, _, width, by_cols in plan for shape in TorusSum.scratch(rows, width, by_cols)]


def plan_sums(grads, plans, refs, in_vmem=False):
    groups = []
    for grad, plan in zip(grads, plans):
        groups.append([])
        for order, rows, col, width, by_cols in plan:
            groups[-1].append(TorusSum(grad, order, rows, col, width, refs[:TorusSum.COUNT], by_cols, in_vmem))
            refs = refs[TorusSum.COUNT:]
    return groups


PLAN_UP = plan_columns(16, (5, 5, 6))
PLAN_DOWN = plan_columns(32, (3, 3, 2))
PLAN_QKV = plan_columns(16, (4, 4, 4))
PLAN_OUT = plan_columns(8, (2, 2, 4), True)


def normed(x):
    x = x.astype(F32)
    centered = x - jnp.mean(x, axis=-1, keepdims=True)
    rstd = lax.rsqrt(jnp.mean(centered * centered, axis=-1, keepdims=True) + NORM_EPS)
    return centered * rstd, rstd


def token_kernel(x_hbm, dy_hbm, ln_ref, wqkv_hbm, wout_hbm, wup_hbm, wdown_hbm,
                 ha_ref, qkv_ref, dctx_ref, dhm_ref, dy_ref, gup_ref, gdown_ref,
                 xs, dys, wqkv, wout, wup, wdown, ha_s, hm_s, hm_t, dh_s, up_acc, down_acc,
                 row_load, w_load, chunk_load, flush_sem, dy_sem, send, recv):
    step = pl.program_id(0)
    first, last = step == 0, step == pl.num_programs(0) - 1
    width = wup.shape[1]
    chunks = width // FC
    rows = pl.ds(pl.multiple_of(step * TT, TT), TT)

    def chunk(c):
        return pl.ds(pl.multiple_of(c * FC, FC), FC)

    def flush(c):
        return (pltpu.make_async_copy(up_acc.at[:, chunk(c)], gup_ref.at[:, chunk(c)], flush_sem.at[0, c]),
                pltpu.make_async_copy(down_acc.at[chunk(c), :], gdown_ref.at[chunk(c), :], flush_sem.at[1, c]))

    def row_loads(n):
        part = pl.ds(n * TT, TT)
        return [pltpu.make_async_copy(src.at[part], dst.at[part], row_load.at[k, n]) for k, (src, dst) in enumerate(((x_hbm, xs), (dy_hbm, dys)))]

    def chunk_loads(c):
        return (pltpu.make_async_copy(wup_hbm.at[:, chunk(c)], wup.at[:, chunk(c)], chunk_load.at[0, c]),
                pltpu.make_async_copy(wdown_hbm.at[chunk(c), :], wdown.at[chunk(c), :], chunk_load.at[1, c]))

    core = lax.axis_index('tp')
    dy_saves = [pltpu.make_async_copy(dys.at[pl.ds(n * HALF, HALF)], dy_ref.at[pl.ds(place * HALF, HALF)], dy_sem.at[n])
                for n, place in enumerate((core, 1 - core))]
    w_loads = [pltpu.make_async_copy(src, dst, w_load.at[k]) for k, (src, dst) in enumerate(((wqkv_hbm, wqkv), (wout_hbm, wout)))]
    swaps = [send_to(other_core(), src, dst.at[pl.ds(HALF, HALF)], send.at[k], recv.at[k]) for k, (src, dst) in enumerate(((x_hbm, xs), (dy_hbm, dys)))]

    @pl.when(first)
    def _():
        for copy in [*row_loads(0), *(copy for c in range(chunks) for copy in chunk_loads(c)), *w_loads, *row_loads(1)]:
            copy.start()
        up_acc[:] = jnp.zeros_like(up_acc)
        down_acc[:] = jnp.zeros_like(down_acc)
        greet([other_core()])
        for copy in swaps:
            copy.start()

    def norms(n):
        norm, _ = normed(xs[pl.ds(pl.multiple_of(n * TT, TT), TT), :])
        hm = (norm * ln_ref[pl.ds(2, 1), :] + ln_ref[pl.ds(3, 1), :]).astype(BF16)
        ha_s[:] = (norm * ln_ref[pl.ds(0, 1), :] + ln_ref[pl.ds(1, 1), :]).astype(BF16).T
        hm_s[:] = hm
        hm_t[:] = hm.T

    @pl.when(first)
    def _():
        for copy in row_loads(0):
            copy.wait()
        norms(0)

    ha_ref[:] = ha_s[:]

    def columns(c, carry):
        @pl.when(first)
        def _():
            for copy in chunk_loads(c):
                copy.wait()
        cols = chunk(c)
        u = dot(hm_s[:], wup[:, cols]).astype(BF16).astype(F32)
        dg = dot_nt(dys[rows, :], wdown[cols, :]).astype(BF16).astype(F32)
        cdf = 0.5 * (1.0 + lax.erf(u * math.sqrt(0.5)))
        gelu = (u * cdf).astype(BF16)
        pdf = jnp.exp(-0.5 * u * u) * (1.0 / math.sqrt(2.0 * math.pi))
        dh = (dg * (cdf + u * pdf)).astype(BF16)
        dh_s[:, cols] = dh
        down_acc[cols, :] += dot(gelu.T, dys[rows, :])
        up_acc[:, cols] += dot(hm_t[:], dh)

        @pl.when(last)
        def _():
            for copy in flush(c):
                copy.start()
        return carry
    lax.fori_loop(0, chunks, columns, 0)
    @pl.when(first)
    def _():
        for copy in w_loads:
            copy.wait()
    for n in range(1, HALF // TT):
        @pl.when(step == n - 1)
        def _(n=n):
            for copy in row_loads(n):
                copy.wait()

    @pl.when(step == HALF // TT - 1)
    def _():
        for copy in swaps:
            copy.wait_recv()
        for copy in dy_saves:
            copy.start()

    dhm_ref[:] = dot_nt(dh_s[:], wup[:]).astype(BF16)
    norms(jnp.minimum(step + 1, pl.num_programs(0) - 1))
    qkv_ref[:] = dot(wqkv[:], ha_ref[:]).astype(BF16)
    dctx_ref[:] = dot_nt(wout[:], dys[rows, :]).astype(BF16)

    @pl.when(last)
    def _():
        for copy in swaps:
            copy.wait_send()
        for copy in dy_saves:
            copy.wait()
        for c in range(chunks):
            for copy in flush(c):
                copy.wait()


def token_part(x, dy, ln, wqkv_t, wout, wup, wdown):
    D, width = wup.shape
    S, V, dma = jax.ShapeDtypeStruct, pltpu.VMEM, pltpu.SemaphoreType.DMA
    hbm = pl.BlockSpec(memory_space=pl.ANY)
    steps, halves = T // TT, HALF // TT

    def tile(i):
        core = lax.axis_index('tp')
        return jnp.where(i < halves, core * halves + i, (1 - core) * halves + i - halves)

    def tok(size):
        return pl.BlockSpec((TT, size), lambda i: (tile(i), 0))

    def col(size):
        return pl.BlockSpec((size, TT), lambda i: (0, tile(i)))

    return pl.pallas_call(
        token_kernel,
        grid=(steps,),
        in_specs=[hbm, hbm, pl.BlockSpec(memory_space=pltpu.VMEM)] + [hbm] * 4,
        out_specs=[col(D), col(wqkv_t.shape[0]), col(wout.shape[0]), tok(D), hbm, hbm, hbm],
        out_shape=[S((D, T), BF16), S((wqkv_t.shape[0], T), BF16), S((wout.shape[0], T), BF16), S((T, D), BF16), S((T, D), BF16),
                   S((D, width), F32), S((width, D), F32)],
        scratch_shapes=[V((T, D), BF16)] * 2 + [V(w.shape, BF16) for w in (wqkv_t, wout, wup, wdown)]
        + [V((D, TT), BF16), V((TT, D), BF16), V((D, TT), BF16), V((TT, width), BF16), V((D, width), F32), V((width, D), F32)]
        + [dma((2, halves)), dma((2,)), dma((2, width // FC)), dma((2, width // FC)), dma((2,)), dma((2,)), dma((2,))],
        compiler_params=pltpu.CompilerParams(dimension_semantics=("arbitrary",), vmem_limit_bytes=VMEM_LIMIT,
                                             collective_id=2, has_side_effects=True),
        cost_estimate=pl.CostEstimate(flops=52 * 10**9, bytes_accessed=60 << 20, transcendentals=2 * T * width),
        name="token_part",
    )(x, dy, ln, wqkv_t, wout, wup, wdown)


def attention_pair(qkv_ref, dctx_ref, cos_ref, sin_ref, dqkv_ref, ctx_ref, q_t, k_t, q_n, k_n, v_n, do_n, p_s, dp_s, dk_acc, dv_acc, slot):
    lane = lax.broadcasted_iota(jnp.int32, (TILE, PAIR), 1)
    key = lax.broadcasted_iota(jnp.int32, (TILE, 2 * TILE), 0)
    query = lax.broadcasted_iota(jnp.int32, (TILE, 2 * TILE), 1) % TILE

    def tile_at(j):
        return pl.ds(j * TILE, TILE)

    def head_rows(head, part):
        return pl.ds((3 * head + part) * HEAD, HEAD)

    def halves(x):
        return x[:HEAD // 2].astype(F32), x[HEAD // 2:].astype(F32)

    def rotate(x, cols, sign):
        cos, sin = cos_ref[:, cols], sin_ref[:, cols] * sign
        lo, hi = halves(x)
        return jnp.concatenate([lo * cos - hi * sin, hi * cos + lo * sin], axis=0).astype(BF16)

    def prepare(j):
        cols = tile_at(j)
        for head in range(2):
            rows = pl.ds(head * HEAD, HEAD)
            q_t[rows, cols] = rotate(qkv_ref[head_rows(head, 0), cols], cols, 1.0) * jnp.asarray(HEAD ** -0.5, BF16)
            k_t[rows, cols] = rotate(qkv_ref[head_rows(head, 1), cols], cols, 1.0)
        q_n[cols, :] = q_t[:, cols].T
        k_n[cols, :] = k_t[:, cols].T
        v_n[cols, :] = jnp.concatenate([qkv_ref[head_rows(head, 2), cols] for head in range(2)], axis=0).T
        do_n[cols, :] = dctx_ref[:, cols].T

    def split_lanes(x):
        zero = jnp.zeros_like(x)
        return jnp.concatenate([jnp.where(lane < HEAD, x, zero), jnp.where(lane < HEAD, zero, x)], axis=0)

    def split_rows(x):
        zero = jnp.zeros((HEAD, TILE), x.dtype)
        return jnp.concatenate([jnp.concatenate([x[:HEAD], zero], axis=1), jnp.concatenate([zero, x[HEAD:]], axis=1)], axis=0)

    def fold(x, op):
        parts = [x[r:r + 8] for r in range(0, TILE, 8)]
        while len(parts) > 1:
            parts = [op(a, b) for a, b in zip(parts[::2], parts[1::2])]
        return parts[0]

    def gather(old, new, op):
        return new if old is None else op(old, new)

    blocks = list(reversed(range(T // TILE)))
    before = {i: sum(b + 1 for b in blocks[:n]) for n, i in enumerate(blocks)}

    def p_at(i, j):
        return pl.ds((before[i] + j) % P_TILES * TILE, TILE)

    def dp_at(i, j):
        return pl.ds((before[i] + j) % DP_TILES * TILE, TILE)

    def scores(i, state):
        q_split = split_rows(q_t[:, tile_at(i)])
        top = None
        for j in range(i + 1):
            s = dot(k_n[tile_at(j), :], q_split)
            if j == i:
                s = jnp.where(query >= key, s, -1e30)
            p_s[p_at(i, j), :] = s
            top = gather(top, fold(s, jnp.maximum), jnp.maximum)
            if j == i:
                state['max'] = jnp.max(top, axis=0, keepdims=True)
            yield

    def weights(i, state):
        do_split = split_rows(dctx_ref[:, tile_at(i)])
        total = both = None
        for j in range(i + 1):
            dp = dot(v_n[tile_at(j), :], do_split).astype(BF16)
            dp_s[dp_at(i, j), :] = dp
            p = jnp.exp2((p_s[p_at(i, j), :] - state['max']) * LOG2E)
            p_s[p_at(i, j), :] = p
            total = gather(total, fold(p, jnp.add), jnp.add)
            both = gather(both, fold(p * dp.astype(F32), jnp.add), jnp.add)
            if j == i:
                state['inv'] = 1.0 / jnp.sum(total, axis=0, keepdims=True)
                state['delta'] = jnp.sum(both, axis=0, keepdims=True) * state['inv']
            yield

    def grads(i, state):
        cols = tile_at(i)
        q_pair, do_pair = split_lanes(q_n[cols, :]), split_lanes(do_n[cols, :])
        ctx, dq = [None] * 2, [None] * 2
        for j in range(i + 1):
            keys = tile_at(j)
            p = p_s[p_at(i, j), :] * state['inv']
            p_bf = p.astype(BF16)
            ds_bf = (p * (dp_s[dp_at(i, j), :].astype(F32) - state['delta'])).astype(BF16)
            for head in range(2):
                side = slice(head * TILE, (head + 1) * TILE)
                ctx[head] = gather(ctx[head], dot(qkv_ref[head_rows(head, 2), keys], p_bf[:, side]), jnp.add)
                dq[head] = gather(dq[head], dot(k_t[pl.ds(head * HEAD, HEAD), keys], ds_bf[:, side]), jnp.add)
            for acc, new in ((dv_acc, dot(p_bf, do_pair)), (dk_acc, dot(ds_bf, q_pair))):
                acc[keys, :] = new if i == blocks[0] else acc[keys, :] + new
            if j == i:
                dk, dv = dk_acc[cols, :].astype(BF16).T, dv_acc[cols, :].astype(BF16).T
                for head in range(2):
                    rows = pl.ds(head * HEAD, HEAD)
                    side = slice(head * HEAD, (head + 1) * HEAD)
                    ctx_ref[rows, cols] = ctx[head].astype(BF16)
                    dqkv_ref[head_rows(head, 0), cols] = rotate((dq[head] * HEAD ** -0.5).astype(BF16), cols, -1.0)
                    dqkv_ref[head_rows(head, 1), cols] = rotate(dk[side], cols, -1.0)
                    dqkv_ref[head_rows(head, 2), cols] = dv[side]
            yield

    slot(0)
    for j in range(T // TILE):
        prepare(j)
    states = {i: {} for i in blocks}
    for n in range(len(blocks) + 2):
        work = []
        for stage, make in ((n - 2, grads), (n - 1, weights), (n, scores)):
            if 0 <= stage < len(blocks):
                i = blocks[stage]
                run = make(i, states[i])
                work += [((j + 0.5) / (i + 1), run) for j in range(i + 1)]
        for _, run in sorted(work, key=lambda item: item[0]):
            next(run)
        if n in SLOT_AFTER:
            slot(SLOT_AFTER[n])


P_TILES, DP_TILES = 21, 15
SLOT_AFTER = {2: 1, 4: 2, 6: 3, 9: 4}
HEAD, PAIR = 64, 128


def attention_scratch():
    V = pltpu.VMEM
    return [V((PAIR, T), BF16)] * 2 + [V((T, PAIR), BF16)] * 4 + [V((P_TILES * TILE, 2 * TILE), F32), V((DP_TILES * TILE, 2 * TILE), BF16)] \
        + [V((T, PAIR), F32)] * 2


SCHEDULE = {
    (0, 0): (('start', 0),),
    (1, 3): (('add', 0), ('pass_on', 0)),
    (2, 3): (('finish', 0), ('start', 1)),
    (3, 1): (('add', 1), ('pass_on', 1)),
    (3, 2): (('finish', 1), ('start', 2)),
    (3, 3): (('add', 2), ('pass_on', 2)),
    (3, 4): (('finish', 2),),
}


def attention_kernel(qkv_ref, dctx_ref, cos_ref, sin_ref, up_ref, down_ref, dqkv_ref, ctx_ref, up_out, down_out, *refs):
    count = len(attention_scratch())
    groups = plan_sums((up_ref, down_ref), (PLAN_UP, PLAN_DOWN), refs[count:])
    every = groups[0] + groups[1]

    def slot(place):
        for (pair, at), stages in SCHEDULE.items():
            if at != place:
                continue

            @pl.when(pl.program_id(0) == pair)
            def _(pair=pair, stages=stages):
                if (pair, place) == (0, 0):
                    greet([ring_chip(axis, ahead) for axis in AXES for ahead in (1, 3)])
                for stage, phase in stages:
                    for one in every:
                        getattr(one, stage)(phase)
                if (pair, place) == list(SCHEDULE)[-1]:
                    for out, sums in zip((up_out, down_out), groups):
                        for one in sums:
                            out[:, one.cols] = one.result[:]
                            one.drain()

    attention_pair(qkv_ref, dctx_ref, cos_ref, sin_ref, dqkv_ref, ctx_ref, *refs[:count], slot)


def attention(qkv_t, dctx_t, cos_t, sin_t, g_up, g_down):
    pairs = dctx_t.shape[0] // PAIR
    S = jax.ShapeDtypeStruct
    shares = [(g.shape[0] // 64, g.shape[1]) for g in (g_up, g_down)]
    hbm = pl.BlockSpec(memory_space=pl.ANY)

    def by_pair(rows):
        return pl.BlockSpec((rows, T), lambda p: (p, 0))

    def fixed(shape):
        return pl.BlockSpec(shape, lambda p: (0, 0), pipeline_mode=pl.Buffered(1))

    return pl.pallas_call(
        attention_kernel,
        grid=(pairs,),
        in_specs=[by_pair(3 * PAIR), by_pair(PAIR), fixed(cos_t.shape), fixed(sin_t.shape), hbm, hbm],
        out_specs=[by_pair(3 * PAIR), by_pair(PAIR)] + [fixed(share) for share in shares],
        out_shape=[S(qkv_t.shape, BF16), S(dctx_t.shape, BF16)] + [S(share, F32) for share in shares],
        scratch_shapes=attention_scratch() + plan_scratch((PLAN_UP, PLAN_DOWN)),
        compiler_params=pltpu.CompilerParams(dimension_semantics=("arbitrary",), vmem_limit_bytes=VMEM_LIMIT,
                                             collective_id=0, has_side_effects=True),
        cost_estimate=pl.CostEstimate(flops=80 * 10**9, bytes_accessed=20 << 20, transcendentals=8 * T * T // 2),
        name="attention",
    )(qkv_t, dctx_t, cos_t, sin_t, *(g.reshape((RING,) * 3 + (-1, g.shape[1])) for g in (g_up, g_down)))


def tail_kernel(hat_hbm, dqkv_hbm, ctx_hbm, dy_hbm, w_hbm, x_hbm, dhm_hbm, ln_ref, gx_ref, gln_ref, gqkv_ref, gout_ref,
                hat, dqkv, ctx, dy, w, x, dhm_own, dhm_in, dha_s, dha_in, g_qkv, g_out, pair_s, ring_s,
                load, send, recv, ring_send, ring_recv, *sum_refs):
    core = lax.axis_index('tp')
    own, away = core * HALF, (1 - core) * HALF
    qkv_sums, out_sums = plan_sums((g_qkv, g_out), (PLAN_QKV, PLAN_OUT), sum_refs, True)
    every = qkv_sums + out_sums
    block = dqkv.shape[0] // len(qkv_sums)

    def rows_of(ref, start, size):
        return ref.at[pl.ds(start, size)]

    pieces = [(hat_hbm, hat)] + [(rows_of(dqkv_hbm, n * block, block), rows_of(dqkv, n * block, block)) for n in range(3)]
    pieces += [(ctx_hbm, ctx), (dy_hbm, dy), (w_hbm, w), (x_hbm, x), (rows_of(dhm_hbm, own, HALF), dhm_own)]
    loads = [pltpu.make_async_copy(src, dst, load.at[n]) for n, (src, dst) in enumerate(pieces)]
    for copy in loads:
        copy.start()
    greet([ring_chip(axis, ahead) for axis in AXES for ahead in (1, 2, 3)] + [other_core()])
    dhm_copy = send_to(other_core(), rows_of(dhm_hbm, away, HALF), dhm_in, send.at[0], recv.at[0])
    dha_copy = send_to(other_core(), dha_s.at[0], dha_in, send.at[1], recv.at[1])
    pair_copy = send_to(other_core(), pair_s.at[0], pair_s.at[1], send.at[2], recv.at[2])
    dhm_copy.start()

    loads[0].wait()
    per_group = block // TILE

    def columns(k, carry):
        for n in range(len(qkv_sums)):
            @pl.when(k == n * per_group)
            def _(n=n):
                loads[1 + n].wait()
        cols = pl.ds(pl.multiple_of(k * TILE, TILE), TILE)
        g_qkv[:, :, :, :, cols] = dot_nt(hat[:], dqkv[cols, :]).reshape(g_qkv.shape[:4] + (TILE,))
        for n, one in enumerate(qkv_sums):
            @pl.when(k == (n + 1) * per_group - 1)
            def _(one=one):
                one.start(0)
        return carry
    lax.fori_loop(0, len(qkv_sums) * per_group, columns, 0)
    loads[4].wait()
    loads[5].wait()

    def out_columns(k, carry):
        cols = pl.ds(pl.multiple_of(k * TILE, TILE), TILE)
        g_out[:, :, :, :, cols] = dot(ctx[:], dy[:, cols]).reshape(g_out.shape[:4] + (TILE,))
        return carry
    lax.fori_loop(0, dy.shape[1] // TILE, out_columns, 0)
    for one in out_sums:
        one.start(0)

    loads[6].wait()
    tiles = HALF // TILE

    def tokens(k, carry):
        mine = lax.div(k, tiles)
        at = lax.rem(k, tiles) * TILE
        cols = pl.ds(pl.multiple_of(jnp.where(mine == 0, away, own) + at, TILE), TILE)
        dha_s[mine, pl.ds(pl.multiple_of(at, TILE), TILE), :] = dot(dqkv[:, cols].T, w[:]).astype(BF16)

        @pl.when(k == tiles - 1)
        def _():
            dha_copy.start()
        return carry
    lax.fori_loop(0, 2 * tiles, tokens, 0)

    def stages(sums, phase, *names):
        for name in names:
            for one in sums:
                getattr(one, name)(phase)

    stages(qkv_sums, 0, 'add', 'pass_on')
    loads[7].wait()
    loads[8].wait()
    dhm_copy.wait_recv()
    dha_copy.wait_recv()
    pair_s[0] = jnp.zeros_like(pair_s[0])

    def norm_back(k, carry):
        at = pl.ds(pl.multiple_of(k * SMALL, SMALL), SMALL)
        norm, rstd = normed(x[at, :])
        da = (dha_s[1, at, :].astype(F32) + dha_in[at, :].astype(F32)).astype(BF16).astype(F32)
        dm = (dhm_own[at, :].astype(F32) + dhm_in[at, :].astype(F32)).astype(BF16).astype(F32)
        g = da * ln_ref[pl.ds(0, 1), :] + dm * ln_ref[pl.ds(2, 1), :]
        mean_g = jnp.mean(g, axis=-1, keepdims=True)
        mean_gn = jnp.mean(g * norm, axis=-1, keepdims=True)
        residual = dy[pl.ds(pl.multiple_of(own + k * SMALL, SMALL), SMALL), :].astype(F32)
        gx_ref[at, :] = (residual + rstd * (g - mean_g - norm * mean_gn)).astype(BF16)
        for row, value in enumerate((da * norm, da, dm * norm, dm)):
            pair_s[0, pl.ds(row, 1), :] += jnp.sum(value, axis=0, keepdims=True)
        return carry

    steps = HALF // SMALL

    def norm_step(k, carry):
        @pl.when(k == steps // 2)
        def _():
            stages(out_sums, 0, 'add', 'pass_on')
            stages(qkv_sums, 0, 'finish')
            stages(qkv_sums, 1, 'start')
        return norm_back(k, carry)
    lax.fori_loop(0, steps, norm_step, 0)
    pair_copy.start()
    stages(out_sums, 0, 'finish')
    stages(out_sums, 1, 'start')
    stages(qkv_sums, 1, 'add', 'pass_on')
    stages(out_sums, 1, 'add', 'pass_on')

    def ring_copies(phase):
        place = ring_place(AXES[phase])
        return [send_to(ring_chip(AXES[phase], ahead), ring_s.at[phase, place], ring_s.at[phase, place],
                        ring_send.at[phase, ahead], ring_recv.at[phase, ahead]) for ahead in (1, 2, 3)]

    def ring_start(phase, value):
        ring_s[phase, ring_place(AXES[phase])] = value
        for copy in ring_copies(phase):
            copy.start()

    def ring_sum(phase):
        for copy in ring_copies(phase):
            copy.wait_recv()
        return ring_s[phase, 0] + ring_s[phase, 1] + ring_s[phase, 2] + ring_s[phase, 3]

    pair_copy.wait_recv()
    ring_start(0, pair_s[0] + pair_s[1])
    stages(every, 1, 'finish')
    stages(every, 2, 'start')
    ring_start(1, ring_sum(0))
    stages(every, 2, 'add', 'pass_on')
    ring_start(2, ring_sum(1))
    stages(every, 2, 'finish')
    gln_ref[:] = ring_sum(2)[:gln_ref.shape[0]]
    for out, sums in ((gqkv_ref, qkv_sums), (gout_ref, out_sums)):
        for one in sums:
            out[:, one.cols] = one.result[:]
            one.drain()
    for copy in (dhm_copy, dha_copy, pair_copy):
        copy.wait_send()
    for phase in range(3):
        for copy in ring_copies(phase):
            copy.wait_send()


def tail(ha_t, dqkv_t, ctx_t, dy, wqkv_t, x, dhm, ln):
    D, C = ha_t.shape[0], ctx_t.shape[0]
    S, V = jax.ShapeDtypeStruct, pltpu.VMEM
    hbm, vmem = pl.BlockSpec(memory_space=pl.ANY), pl.BlockSpec(memory_space=pltpu.VMEM)
    own = V((HALF, D), BF16)
    chips = (RING,) * 3
    dma = pltpu.SemaphoreType.DMA
    return pl.pallas_call(
        tail_kernel,
        in_specs=[hbm] * 7 + [vmem],
        out_specs=[vmem] * 4,
        out_shape=[S((HALF, D), BF16), S(ln.shape, F32), S((D // 64, 3 * C), F32), S((C // 64, D), F32)],
        scratch_shapes=[V(a.shape, BF16) for a in (ha_t, dqkv_t, ctx_t, dy, wqkv_t)] + [own] * 3 + [V((2, HALF, D), BF16), own]
        + [V(chips + (D // 64, 3 * C), F32), V(chips + (C // 64, D), F32), V((2, 8, D), F32), V((3, RING, 8, D), F32)]
        + [dma((9,)), dma((3,)), dma((3,)), dma((3, RING)), dma((3, RING))] + plan_scratch((PLAN_QKV, PLAN_OUT)),
        compiler_params=pltpu.CompilerParams(vmem_limit_bytes=VMEM_LIMIT, collective_id=1, has_side_effects=True),
        cost_estimate=pl.CostEstimate(flops=15 * 10**9, bytes_accessed=30 << 20, transcendentals=0),
        name="tail",
    )(ha_t, dqkv_t, ctx_t, dy, wqkv_t, x, dhm, ln)


def output_kernel(*refs):
    ins, outs = refs[:len(refs) // 2], refs[len(refs) // 2:]
    outs[0][:] = ins[0][:]

    @pl.when(pl.program_id(0) == 0)
    def _():
        for src, dst in zip(ins[2:], outs[2:]):
            dst[:] = src[:]
        wide, split = ins[1], outs[1]
        for group in range(split.shape[2]):
            for part in range(3):
                split[:, part, group, :] = wide[:, pl.ds((3 * group + part) * HEAD, HEAD)]


def outputs(grad_x, grad_wqkv, *rest):
    rows, cols = grad_wqkv.shape
    split = jax.ShapeDtypeStruct((rows, 3, cols // (3 * HEAD), HEAD), F32)
    shapes = [grad_x, split, *rest]
    steps = 4

    def fixed(a):
        return pl.BlockSpec(a.shape, lambda i: (0,) * len(a.shape), pipeline_mode=pl.Buffered(1))

    tok = pl.BlockSpec((grad_x.shape[0] // steps, grad_x.shape[1]), lambda i: (i, 0))
    return pl.pallas_call(
        output_kernel, grid=(steps,),
        in_specs=[tok, fixed(grad_wqkv)] + [fixed(a) for a in rest],
        out_specs=[tok, fixed(split)] + [fixed(a) for a in rest],
        out_shape=[jax.ShapeDtypeStruct(a.shape, a.dtype) for a in shapes],
        compiler_params=pltpu.CompilerParams(dimension_semantics=("arbitrary",)),
        name="outputs",
    )(grad_x, grad_wqkv, *rest)


def solution(mesh):
    def local_step(x_loc, dy_loc, ln_params, w_qkv, w_out, w_up, w_down):
        x_loc, dy_loc = x_loc[0], dy_loc[0]
        wqkv_t = w_qkv.transpose(1, 2, 3, 0).reshape(-1, x_loc.shape[1])
        cos_t, sin_t = rope_tables()
        ha_t, qkv_t, dctx_t, dhm, dy, g_wup, g_wdown = token_part(x_loc, dy_loc, ln_params, wqkv_t, w_out, w_up, w_down)
        dqkv_t, ctx_t, grad_wup, grad_wdown = attention(qkv_t, dctx_t, cos_t, sin_t, g_wup, g_wdown)
        grad_x, grad_ln, grad_wqkv, grad_wout = tail(ha_t, dqkv_t, ctx_t, dy, wqkv_t, x_loc, dhm, ln_params)
        grad_x, grad_wqkv, *rest = outputs(grad_x, grad_wqkv, grad_ln, grad_wout, grad_wup, grad_wdown)
        return grad_x[None], rest[0], grad_wqkv.swapaxes(1, 2), *rest[1:]

    act_spec = P('dp', 'tp')
    in_specs = (act_spec, act_spec, P(), P(None, 'tp'), P('tp'), P(None, 'tp'), P('tp'))
    out_specs = (act_spec, P(), P('dp', 'tp'), P(('tp', 'dp')), P('dp', 'tp'), P(('tp', 'dp')))
    return jax.shard_map(local_step, mesh=mesh, in_specs=in_specs, out_specs=out_specs, check_vma=False)
```

profile of v0, /device:TPU:0, one launch (start us, length us, event | category | flops | bytes accessed | tf_op | source)
XLA Modules:
  0.0 219.6 jit_solution(12692255909224411264)
XLA Ops:
  0.6 1.8 fusion
  2.5 65.9 %token_part.1 = (bf16[1024,2048]{1,0:T(8,128)(2,1)}, bf16[1536,2048]{1,0:T(8,128)(2,1)}, bf16[512,2048]{1,0:T(8,128)(2,1)}, bf16[2048,1024]{1,0:T(8,128)(2,1)}, ...) custom-call(bf16[1024,1024]{1,0:T(8,128)(2,1)} %bitcast.12, bf16[1024,1024]{1,0:T(8,128)(2,1)} %bitcast.11, ...), custom_call_target="tpu_custom_call" | custom-call | flops 51999997952 | bytes 62914560 | tf_op jit(solution)/shard_map/token_part/pallas_call | solution.py:342
  68.4 85.7 %attention.1 = (bf16[1536,2048]{1,0:T(8,128)(2,1)}, bf16[512,2048]{1,0:T(8,128)(2,1)}, f32[16,2048]{1,0:T(8,128)}, f32[32,1024]{1,0:T(8,128)}) custom-call(bf16[1536,2048]{1,0:T(8,128)(2,1)} %get-tuple-element.28.qkv_ref, bf16[512,2048]{1,0:T(8,128)(2,1)} %get-tuple-element.29.dctx_ref, f32[32,2048]{1,0:T(8,128)} %get-tuple-element.49.cos_ref, ...), custom_call_target="tpu_custom_call" | custom-call | flops 80000000000 | bytes 20971520 | tf_op jit(solution)/shard_map/attention/pallas_call | solution.py:546
  154.1 61.0 %tail.1 = (bf16[1024,1024]{1,0:T(8,128)(2,1)}, f32[4,1024]{1,0:T(4,128)}, f32[16,1536]{1,0:T(8,128)}, f32[8,1024]{1,0:T(8,128)}) custom-call(bf16[1024,2048]{1,0:T(8,128)(2,1)} %get-tuple-element.27.hat_hbm, bf16[1536,2048]{1,0:T(8,128)(2,1)} %get-tuple-element.32.dqkv_hbm, bf16[512,2048]{1,0:T(8,128)(2,1)} %get-tuple-element.33.ctx_hbm, ...), custom_call_target="tpu_custom_call" | custom-call | flops 15000000512 | bytes 31457280 | tf_op jit(solution)/shard_map/tail/pallas_call | solution.py:709
  215.1 4.4 %outputs.1 = (bf16[1024,1024]{1,0:T(8,128)(2,1)}, f32[16,3,8,64]{3,2,1,0:T(8,128)}, f32[4,1024]{1,0:T(4,128)}, f32[8,1024]{1,0:T(8,128)}, f32[16,2048]{1,0:T(8,128)}, /*index=5*/f32[32,1024]{1,0:T(8,128)}) custom-call(bf16[1024,1024]{1,0:T(8,128)(2,1)} %get-tuple-element.36.refs_0_, f32[16,1536]{1,0:T(8,128)} %get-tuple-element.37.refs_1_, ...), custom_call_target="tpu_custom_call" | custom-call | tf_op jit(solution)/shard_map/outputs/pallas_call | solution.py:747
  (1 shorter events, 0.0 us)
where the time goes:
time: 220 us
  Pallas kernels  217 us (99%)
    pallas_call x1, Pallas kernels, attention(): pl.pallas_call(attention_kernel, grid=(pairs,), in_specs=[by_pair(3 * PAI...  85.7 us
    pallas_call x1, Pallas kernels, token_part(): pl.pallas_call(token_kernel, grid=(steps,), in_specs=[hbm, hbm, pl.BlockS...  65.9 us
    pallas_call x1, Pallas kernels, tail(): pl.pallas_call(tail_kernel, in_specs=[hbm] * 7 + [vmem], out_specs=[vmem]...  61 us

commit v1 on v0

--- a/solution.py
+++ b/solution.py
@@ -19,6 +19,7 @@
 TT = 512
 FC = 1024
 LANES = 128
+HEAD, PAIR = 64, 128
 VMEM_LIMIT = 63 << 20
 AXES = ('z', 'y', 'x')
 AXIS_STRIDE = {'z': 16, 'y': 4, 'x': 1}
@@ -31,12 +32,6 @@
 
 def dot_nt(a, b):
     return lax.dot_general(a, b, (((1,), (1,)), ((), ())), preferred_element_type=F32)
-
-
-def rope_tables():
-    inv_freq = ROPE_BASE ** (-2.0 * jnp.arange(32, dtype=F32) / 64)
-    angles = inv_freq[:, None] * jnp.arange(T, dtype=F32)[None, :]
-    return jnp.cos(angles), jnp.sin(angles)
 
 
 def ring_place(axis):
@@ -202,7 +197,7 @@
 PLAN_UP = plan_columns(16, (5, 5, 6))
 PLAN_DOWN = plan_columns(32, (3, 3, 2))
 PLAN_QKV = plan_columns(16, (4, 4, 4))
-PLAN_OUT = plan_columns(8, (2, 2, 4), True)
+PLAN_OUT = plan_columns(8, (4, 2, 2), True)
 
 
 def normed(x):
@@ -212,8 +207,13 @@
     return centered * rstd, rstd
 
 
-def token_kernel(x_hbm, dy_hbm, ln_ref, wqkv_hbm, wout_hbm, wup_hbm, wdown_hbm,
-                 ha_ref, qkv_ref, dctx_ref, dhm_ref, dy_ref, gup_ref, gdown_ref,
+def token_tile(step):
+    core, halves = lax.axis_index('tp'), HALF // TT
+    return jnp.where(step < halves, core * halves + step, (1 - core) * halves + step - halves)
+
+
+def token_kernel(x_hbm, dy_hbm, ln_ref, freq_ref, wqkv_hbm, wout_hbm, wup_hbm, wdown_hbm,
+                 ha_ref, qkv_ref, dctx_ref, dhm_ref, cos_ref, sin_ref, dy_ref, gup_ref, gdown_ref,
                  xs, dys, wqkv, wout, wup, wdown, ha_s, hm_s, hm_t, dh_s, up_acc, down_acc,
                  row_load, w_load, chunk_load, flush_sem, dy_sem, send, recv):
     step = pl.program_id(0)
@@ -311,6 +311,10 @@
     norms(jnp.minimum(step + 1, pl.num_programs(0) - 1))
     qkv_ref[:] = dot(wqkv[:], ha_ref[:]).astype(BF16)
     dctx_ref[:] = dot_nt(wout[:], dys[rows, :]).astype(BF16)
+    position = token_tile(step) * TT + lax.broadcasted_iota(jnp.int32, cos_ref.shape, 1)
+    angles = position.astype(F32) * freq_ref[:, pl.ds(0, 1)]
+    cos_ref[:] = jnp.cos(angles)
+    sin_ref[:] = jnp.sin(angles)
 
     @pl.when(last)
     def _():
@@ -326,25 +330,23 @@
 def token_part(x, dy, ln, wqkv_t, wout, wup, wdown):
     D, width = wup.shape
     S, V, dma = jax.ShapeDtypeStruct, pltpu.VMEM, pltpu.SemaphoreType.DMA
-    hbm = pl.BlockSpec(memory_space=pl.ANY)
+    hbm, vmem = pl.BlockSpec(memory_space=pl.ANY), pl.BlockSpec(memory_space=pltpu.VMEM)
     steps, halves = T // TT, HALF // TT
-
-    def tile(i):
-        core = lax.axis_index('tp')
-        return jnp.where(i < halves, core * halves + i, (1 - core) * halves + i - halves)
+    freq = np.tile((ROPE_BASE ** (np.arange(0, -HEAD, -2) / HEAD)).astype(np.float32)[:, None], LANES)
 
     def tok(size):
-        return pl.BlockSpec((TT, size), lambda i: (tile(i), 0))
+        return pl.BlockSpec((TT, size), lambda i: (token_tile(i), 0))
 
     def col(size):
-        return pl.BlockSpec((size, TT), lambda i: (0, tile(i)))
+        return pl.BlockSpec((size, TT), lambda i: (0, token_tile(i)))
 
     return pl.pallas_call(
         token_kernel,
         grid=(steps,),
-        in_specs=[hbm, hbm, pl.BlockSpec(memory_space=pltpu.VMEM)] + [hbm] * 4,
-        out_specs=[col(D), col(wqkv_t.shape[0]), col(wout.shape[0]), tok(D), hbm, hbm, hbm],
-        out_shape=[S((D, T), BF16), S((wqkv_t.shape[0], T), BF16), S((wout.shape[0], T), BF16), S((T, D), BF16), S((T, D), BF16),
+        in_specs=[hbm, hbm, vmem, vmem] + [hbm] * 4,
+        out_specs=[col(D), col(wqkv_t.shape[0]), col(wout.shape[0]), tok(D), col(HEAD // 2), col(HEAD // 2), hbm, hbm, hbm],
+        out_shape=[S((D, T), BF16), S((wqkv_t.shape[0], T), BF16), S((wout.shape[0], T), BF16), S((T, D), BF16),
+                   S((HEAD // 2, T), F32), S((HEAD // 2, T), F32), S((T, D), BF16),
                    S((D, width), F32), S((width, D), F32)],
         scratch_shapes=[V((T, D), BF16)] * 2 + [V(w.shape, BF16) for w in (wqkv_t, wout, wup, wdown)]
         + [V((D, TT), BF16), V((TT, D), BF16), V((D, TT), BF16), V((TT, width), BF16), V((D, width), F32), V((width, D), F32)]
@@ -353,7 +355,7 @@
                                              collective_id=2, has_side_effects=True),
         cost_estimate=pl.CostEstimate(flops=52 * 10**9, bytes_accessed=60 << 20, transcendentals=2 * T * width),
         name="token_part",
-    )(x, dy, ln, wqkv_t, wout, wup, wdown)
+    )(x, dy, ln, freq, wqkv_t, wout, wup, wdown)
 
 
 def attention_pair(qkv_ref, dctx_ref, cos_ref, sin_ref, dqkv_ref, ctx_ref, q_t, k_t, q_n, k_n, v_n, do_n, p_s, dp_s, dk_acc, dv_acc, slot):
@@ -485,7 +487,6 @@
 
 P_TILES, DP_TILES = 21, 15
 SLOT_AFTER = {2: 1, 4: 2, 6: 3, 9: 4}
-HEAD, PAIR = 64, 128
 
 
 def attention_scratch():
@@ -557,13 +558,25 @@
     )(qkv_t, dctx_t, cos_t, sin_t, *(g.reshape((RING,) * 3 + (-1, g.shape[1])) for g in (g_up, g_down)))
 
 
+DURING_TOKENS = {2: ('B+0', 'b!0'), 5: ('C+0', 'c!0')}
+DURING_NORMS = {2: ('A=0',), 5: ('B=0', 'a+0'), 7: ('b+0',)}
+AFTER_NORMS = (
+    ('C=0', 'A+1', 'c+0', 'B+1', 'a=0', 'b=0'),
+    ('C+1', 'A=1', 'c=0', 'B=1', 'a+1', 'b+1'),
+    ('A+2', 'B+2', 'C=1', 'c+1', 'a=1', 'b=1'),
+    ('A=2', 'B=2', 'C+2', 'c=1', 'a+2', 'b+2'),
+    ('C=2', 'a=2', 'b=2', 'c+2', 'c=2'),
+)
+
+
 def tail_kernel(hat_hbm, dqkv_hbm, ctx_hbm, dy_hbm, w_hbm, x_hbm, dhm_hbm, ln_ref, gx_ref, gln_ref, gqkv_ref, gout_ref,
                 hat, dqkv, ctx, dy, w, x, dhm_own, dhm_in, dha_s, dha_in, g_qkv, g_out, pair_s, ring_s,
                 load, send, recv, ring_send, ring_recv, *sum_refs):
     core = lax.axis_index('tp')
     own, away = core * HALF, (1 - core) * HALF
-    qkv_sums, out_sums = plan_sums((g_qkv, g_out), (PLAN_QKV, PLAN_OUT), sum_refs, True)
-    every = qkv_sums + out_sums
+    groups = plan_sums((g_qkv, g_out), (PLAN_QKV, PLAN_OUT), sum_refs, True)
+    qkv_sums = groups[0]
+    sums = dict(zip('ABCabc', groups[0] + groups[1]))
     block = dqkv.shape[0] // len(qkv_sums)
 
     def rows_of(ref, start, size):
@@ -579,6 +592,31 @@
     dha_copy = send_to(other_core(), dha_s.at[0], dha_in, send.at[1], recv.at[1])
     pair_copy = send_to(other_core(), pair_s.at[0], pair_s.at[1], send.at[2], recv.at[2])
     dhm_copy.start()
+
+    def run(events):
+        for name, act, ring in events:
+            one, phase = sums[name], int(ring)
+            if act == '!':
+                one.start(phase)
+            elif act == '+':
+                one.add(phase)
+                one.pass_on(phase)
+            else:
+                one.finish(phase)
+                if phase < len(AXES) - 1:
+                    one.start(phase + 1)
+                elif name in 'abc':
+                    gout_ref[:, one.cols] = one.result[:]
+                else:
+                    for k in range(one.whole[1] // HEAD):
+                        group, part = divmod(one.col // HEAD + k, 3)
+                        gqkv_ref[:, part, group, :] = one.result[:, pl.ds(k * HEAD, HEAD)]
+
+    def run_at(k, table):
+        for when, events in table.items():
+            @pl.when(k == when)
+            def _(events=events):
+                run(events)
 
     loads[0].wait()
     per_group = block // TILE
@@ -604,8 +642,7 @@
         g_out[:, :, :, :, cols] = dot(ctx[:], dy[:, cols]).reshape(g_out.shape[:4] + (TILE,))
         return carry
     lax.fori_loop(0, dy.shape[1] // TILE, out_columns, 0)
-    for one in out_sums:
-        one.start(0)
+    run(('A+0', 'a!0'))
 
     loads[6].wait()
     tiles = HALF // TILE
@@ -619,15 +656,10 @@
         @pl.when(k == tiles - 1)
         def _():
             dha_copy.start()
+        run_at(k, DURING_TOKENS)
         return carry
     lax.fori_loop(0, 2 * tiles, tokens, 0)
 
-    def stages(sums, phase, *names):
-        for name in names:
-            for one in sums:
-                getattr(one, name)(phase)
-
-    stages(qkv_sums, 0, 'add', 'pass_on')
     loads[7].wait()
     loads[8].wait()
     dhm_copy.wait_recv()
@@ -651,18 +683,10 @@
     steps = HALF // SMALL
 
     def norm_step(k, carry):
-        @pl.when(k == steps // 2)
-        def _():
-            stages(out_sums, 0, 'add', 'pass_on')
-            stages(qkv_sums, 0, 'finish')
-            stages(qkv_sums, 1, 'start')
+        run_at(k, DURING_NORMS)
         return norm_back(k, carry)
     lax.fori_loop(0, steps, norm_step, 0)
     pair_copy.start()
-    stages(out_sums, 0, 'finish')
-    stages(out_sums, 1, 'start')
-    stages(qkv_sums, 1, 'add', 'pass_on')
-    stages(out_sums, 1, 'add', 'pass_on')
 
     def ring_copies(phase):
         place = ring_place(AXES[phase])
@@ -679,19 +703,16 @@
             copy.wait_recv()
         return ring_s[phase, 0] + ring_s[phase, 1] + ring_s[phase, 2] + ring_s[phase, 3]
 
-    pair_copy.wait_recv()
-    ring_start(0, pair_s[0] + pair_s[1])
-    stages(every, 1, 'finish')
-    stages(every, 2, 'start')
-    ring_start(1, ring_sum(0))
-    stages(every, 2, 'add', 'pass_on')
-    ring_start(2, ring_sum(1))
-    stages(every, 2, 'finish')
+    for n, events in enumerate(AFTER_NORMS):
+        run(events)
+        if n == 0:
+            pair_copy.wait_recv()
+            ring_start(0, pair_s[0] + pair_s[1])
+        elif n < len(AXES):
+            ring_start(n, ring_sum(n - 1))
     gln_ref[:] = ring_sum(2)[:gln_ref.shape[0]]
-    for out, sums in ((gqkv_ref, qkv_sums), (gout_ref, out_sums)):
-        for one in sums:
-            out[:, one.cols] = one.result[:]
-            one.drain()
+    for one in sums.values():
+        one.drain()
     for copy in (dhm_copy, dha_copy, pair_copy):
         copy.wait_send()
     for phase in range(3):
@@ -710,7 +731,7 @@
         tail_kernel,
         in_specs=[hbm] * 7 + [vmem],
         out_specs=[vmem] * 4,
-        out_shape=[S((HALF, D), BF16), S(ln.shape, F32), S((D // 64, 3 * C), F32), S((C // 64, D), F32)],
+        out_shape=[S((HALF, D), BF16), S(ln.shape, F32), S((D // 64, 3, C // HEAD, HEAD), F32), S((C // 64, D), F32)],
         scratch_shapes=[V(a.shape, BF16) for a in (ha_t, dqkv_t, ctx_t, dy, wqkv_t)] + [own] * 3 + [V((2, HALF, D), BF16), own]
         + [V(chips + (D // 64, 3 * C), F32), V(chips + (C // 64, D), F32), V((2, 8, D), F32), V((3, RING, 8, D), F32)]
         + [dma((9,)), dma((3,)), dma((3,)), dma((3, RING)), dma((3, RING))] + plan_scratch((PLAN_QKV, PLAN_OUT)),
@@ -726,44 +747,34 @@
 
     @pl.when(pl.program_id(0) == 0)
     def _():
-        for src, dst in zip(ins[2:], outs[2:]):
+        for src, dst in zip(ins[1:], outs[1:]):
             dst[:] = src[:]
-        wide, split = ins[1], outs[1]
-        for group in range(split.shape[2]):
-            for part in range(3):
-                split[:, part, group, :] = wide[:, pl.ds((3 * group + part) * HEAD, HEAD)]
-
-
-def outputs(grad_x, grad_wqkv, *rest):
-    rows, cols = grad_wqkv.shape
-    split = jax.ShapeDtypeStruct((rows, 3, cols // (3 * HEAD), HEAD), F32)
-    shapes = [grad_x, split, *rest]
-    steps = 4
+
+
+def outputs(grad_x, *rest):
+    steps = 2
 
     def fixed(a):
         return pl.BlockSpec(a.shape, lambda i: (0,) * len(a.shape), pipeline_mode=pl.Buffered(1))
 
-    tok = pl.BlockSpec((grad_x.shape[0] // steps, grad_x.shape[1]), lambda i: (i, 0))
+    specs = [pl.BlockSpec((grad_x.shape[0] // steps, grad_x.shape[1]), lambda i: (i, 0))] + [fixed(a) for a in rest]
     return pl.pallas_call(
-        output_kernel, grid=(steps,),
-        in_specs=[tok, fixed(grad_wqkv)] + [fixed(a) for a in rest],
-        out_specs=[tok, fixed(split)] + [fixed(a) for a in rest],
-        out_shape=[jax.ShapeDtypeStruct(a.shape, a.dtype) for a in shapes],
+        output_kernel, grid=(steps,), in_specs=specs, out_specs=specs,
+        out_shape=[jax.ShapeDtypeStruct(a.shape, a.dtype) for a in (grad_x, *rest)],
         compiler_params=pltpu.CompilerParams(dimension_semantics=("arbitrary",)),
         name="outputs",
-    )(grad_x, grad_wqkv, *rest)
+    )(grad_x, *rest)
 
 
 def solution(mesh):
     def local_step(x_loc, dy_loc, ln_params, w_qkv, w_out, w_up, w_down):
         x_loc, dy_loc = x_loc[0], dy_loc[0]
         wqkv_t = w_qkv.transpose(1, 2, 3, 0).reshape(-1, x_loc.shape[1])
-        cos_t, sin_t = rope_tables()
-        ha_t, qkv_t, dctx_t, dhm, dy, g_wup, g_wdown = token_part(x_loc, dy_loc, ln_params, wqkv_t, w_out, w_up, w_down)
+        ha_t, qkv_t, dctx_t, dhm, cos_t, sin_t, dy, g_wup, g_wdown = token_part(x_loc, dy_loc, ln_params, wqkv_t, w_out, w_up, w_down)
         dqkv_t, ctx_t, grad_wup, grad_wdown = attention(qkv_t, dctx_t, cos_t, sin_t, g_wup, g_wdown)
         grad_x, grad_ln, grad_wqkv, grad_wout = tail(ha_t, dqkv_t, ctx_t, dy, wqkv_t, x_loc, dhm, ln_params)
-        grad_x, grad_wqkv, *rest = outputs(grad_x, grad_wqkv, grad_ln, grad_wout, grad_wup, grad_wdown)
-        return grad_x[None], rest[0], grad_wqkv.swapaxes(1, 2), *rest[1:]
+        grad_x, grad_ln, grad_wqkv, *rest = outputs(grad_x, grad_ln, grad_wqkv, grad_wout, grad_wup, grad_wdown)
+        return grad_x[None], grad_ln, grad_wqkv.swapaxes(1, 2), *rest
 
     act_spec = P('dp', 'tp')
     in_specs = (act_spec, act_spec, P(), P(None, 'tp'), P('tp'), P(None, 'tp'), P('tp'))

time: 220 us -> 214 us (0.973)
  Pallas kernels: 217 us -> 213 us
    pallas_call x1, Pallas kernels: 61 us -> 57.1 us  [tail(): pl.pallas_call(tail_kernel, in_specs=[hbm] * 7 + [vmem], out_specs=[vmem]...]
where the time goes in v1:
time: 214 us
  Pallas kernels  213 us (100%)
    pallas_call x1, Pallas kernels, attention(): pl.pallas_call(attention_kernel, grid=(pairs,), in_specs=[by_pair(3 * PAI...  85.9 us
    pallas_call x1, Pallas kernels, token_part(): pl.pallas_call(token_kernel, grid=(steps,), in_specs=[hbm, hbm, vmem, vme...  67 us
    pallas_call x1, Pallas kernels, tail(): pl.pallas_call(tail_kernel, in_specs=[hbm] * 7 + [vmem], out_specs=[vmem]...  57.1 us

profile of v1, /device:TPU:0, one launch (start us, length us, event | category | flops | bytes accessed | tf_op | source)
XLA Modules:
  0.0 213.7 jit_solution(3545005022727564344)
XLA Ops:
  0.6 67.0 %token_part.1 = (bf16[1024,2048]{1,0:T(8,128)(2,1)}, bf16[1536,2048]{1,0:T(8,128)(2,1)}, bf16[512,2048]{1,0:T(8,128)(2,1)}, bf16[2048,1024]{1,0:T(8,128)(2,1)}, ...) custom-call(bf16[1024,1024]{1,0:T(8,128)(2,1)} %bitcast.12, ...), custom_call_target="tpu_custom_call" | custom-call | flops 51999997952 | bytes 62914560 | tf_op jit(solution)/shard_map/token_part/pallas_call | solution.py:343
  67.6 85.9 %attention.1 = (bf16[1536,2048]{1,0:T(8,128)(2,1)}, bf16[512,2048]{1,0:T(8,128)(2,1)}, f32[16,2048]{1,0:T(8,128)}, f32[32,1024]{1,0:T(8,128)}) custom-call(bf16[1536,2048]{1,0:T(8,128)(2,1)} %get-tuple-element.30.qkv_ref, bf16[512,2048]{1,0:T(8,128)(2,1)} %get-tuple-element.31.dctx_ref, f32[32,2048]{1,0:T(8,128)} %get-tuple-element.32.cos_ref, ...), custom_call_target="tpu_custom_call" | custom-call | flops 80000000000 | bytes 20971520 | tf_op jit(solution)/shard_map/attention/pallas_call | solution.py:547
  153.5 57.1 %tail.1 = (bf16[1024,1024]{1,0:T(8,128)(2,1)}, f32[4,1024]{1,0:T(4,128)}, f32[16,3,8,64]{3,2,1,0:T(8,128)}, f32[8,1024]{1,0:T(8,128)}) custom-call(bf16[1024,2048]{1,0:T(8,128)(2,1)} %get-tuple-element.29.hat_hbm, bf16[1536,2048]{1,0:T(8,128)(2,1)} %get-tuple-element.36.dqkv_hbm, bf16[512,2048]{1,0:T(8,128)(2,1)} %get-tuple-element.37.ctx_hbm, ...), custom_call_target="tpu_custom_call" | custom-call | flops 15000000512 | bytes 31457280 | tf_op jit(solution)/shard_map/tail/pallas_call | solution.py:730
  210.6 2.9 %outputs.1 = (bf16[1024,1024]{1,0:T(8,128)(2,1)}, f32[4,1024]{1,0:T(4,128)}, f32[16,3,8,64]{3,2,1,0:T(8,128)}, f32[8,1024]{1,0:T(8,128)}, f32[16,2048]{1,0:T(8,128)}, /*index=5*/f32[32,1024]{1,0:T(8,128)}) custom-call(bf16[1024,1024]{1,0:T(8,128)(2,1)} %get-tuple-element.40.refs_0_, f32[4,1024]{1,0:T(4,128)} %get-tuple-element.41.refs_1_, ...), custom_call_target="tpu_custom_call" | custom-call | tf_op jit(solution)/shard_map/outputs/pallas_call | solution.py:761

commit v2 on v1

--- a/solution.py
+++ b/solution.py
@@ -60,29 +60,25 @@
 
 
 class TorusSum:
-    COUNT = 30
-
     @staticmethod
     def half_shape(rows, width, by_cols):
         return (rows, width // 2) if by_cols else (rows // 2, width)
 
     @staticmethod
-    def scratch(rows, width, by_cols=False):
+    def scratch(rows, width, by_cols, in_vmem):
         half, whole = TorusSum.half_shape(rows, width, by_cols), (rows, width)
-        shapes = []
-        for lead in ((RING, RING), (RING,), ()):
-            shapes += [pltpu.VMEM(lead + half, F32)] * 8 + [pltpu.VMEM(lead + whole, F32)]
+        leads = ((RING, RING), (RING,), ())
+        shapes = [pltpu.VMEM(lead + shape, F32) for lead in leads for shape in (half,) * 6 + (whole,)]
+        shapes += [] if in_vmem else [pltpu.VMEM(leads[0] + half, F32)] * 2
         return shapes + [pltpu.SemaphoreType.DMA((18,)), pltpu.SemaphoreType.DMA((18,)), pltpu.SemaphoreType.DMA((3,))]
 
-    def __init__(self, grad, order, rows, col, width, refs, by_cols=False, in_vmem=False):
+    def __init__(self, grad, order, rows, col, width, refs, by_cols, in_vmem):
         self.grad, self.order, self.col, self.by_cols, self.in_vmem = grad, order, col, by_cols, in_vmem
         self.whole, self.half = (rows, width), TorusSum.half_shape(rows, width, by_cols)
         self.cols = pl.ds(col, width)
-        self.refs, (self.send, self.recv, self.load) = refs, refs[27:]
+        self.sums = [refs[7 * n:7 * n + 7] for n in range(3)]
+        self.loaded, (self.send, self.recv, self.load) = refs[21:-3], refs[-3:]
         self.kept = [[axis for axis in AXES if axis not in order[:n]] for n in range(3)]
-
-    def bufs(self, phase):
-        return self.refs[9 * phase:9 * phase + 9]
 
     def part(self, which, col=0):
         shape = self.whole if which == 2 else self.half
@@ -96,15 +92,16 @@
         lead = tuple(index if axis == self.order[phase] else slice(None) for axis in self.kept[phase])
         if phase == 0:
             return self.grad.at[lead + self.part(which, self.col)]
-        return self.refs[9 * phase - 1].at[lead + self.part(which)]
+        return self.sums[phase - 1][6].at[lead + self.part(which)]
 
     def load_copy(self, n):
         ahead, which = ((1, 0), (3, 1), (0, 2))[n]
-        return pltpu.make_async_copy(self.block(0, ahead, which), self.bufs(0)[6 + n], self.load.at[n])
+        dst = (*self.loaded, self.sums[0][6])[n]
+        return pltpu.make_async_copy(self.block(0, ahead, which), dst, self.load.at[n])
 
     def copy(self, phase, n):
-        bufs = self.bufs(phase)
-        src = bufs[2 + n] if n >= 4 else self.block(phase, *((2, 0), (1, 1), (2, 1), (3, 0))[n])
+        bufs = self.sums[phase]
+        src = bufs[2 * n - 8] if n >= 4 else self.block(phase, *((2, 0), (1, 1), (2, 1), (3, 0))[n])
         chip = ring_chip(self.order[phase], (1, 1, 3, 3, 1, 3)[n])
         return send_to(chip, src, bufs[n], self.send.at[6 * phase + n], self.recv.at[6 * phase + n])
 
@@ -119,18 +116,18 @@
                 self.load_copy(n).start()
 
     def add(self, phase):
-        bufs = self.bufs(phase)
+        bufs = self.sums[phase]
         own = self.block(phase, 1, 0), self.block(phase, 3, 1)
         if self.loads(phase):
-            own = bufs[6], bufs[7]
+            own = self.loaded
             self.load_copy(0).wait()
             self.load_copy(1).wait()
         self.copy(phase, 0).wait_recv()
         self.copy(phase, 2).wait_recv()
 
         def rows(at):
-            bufs[6][at] = own[0][at] + bufs[0][at]
-            bufs[7][at] = own[1][at] + bufs[2][at]
+            bufs[0][at] = own[0][at] + bufs[0][at]
+            bufs[2][at] = own[1][at] + bufs[2][at]
         self.each(phase, rows)
 
     def each(self, phase, body):
@@ -147,9 +144,9 @@
         self.copy(phase, 5).start()
 
     def finish(self, phase):
-        bufs = self.bufs(phase)
+        bufs = self.sums[phase]
         lead = (slice(None),) * (2 - phase)
-        low, high = bufs[8].at[lead + self.part(0)], bufs[8].at[lead + self.part(1)]
+        low, high = bufs[6].at[lead + self.part(0)], bufs[6].at[lead + self.part(1)]
         own = self.block(phase, 0, 0), self.block(phase, 0, 1)
         if self.loads(phase):
             own = low, high
@@ -169,19 +166,19 @@
 
     @property
     def result(self):
-        return self.refs[26]
+        return self.sums[2][6]
 
 
 def plan_columns(rows, tiles, by_cols=False):
-    plan, col = [], 0
-    for order, count in zip((('x', 'y', 'z'), ('y', 'z', 'x'), ('z', 'x', 'y')), tiles):
-        plan.append((order, rows, col, count * LANES, by_cols))
+    plan, col, orders = [], 0, (('x', 'y', 'z'), ('y', 'z', 'x'), ('z', 'x', 'y'))
+    for n, count in enumerate(tiles):
+        plan.append((orders[n % len(orders)], rows, col, count * LANES, by_cols))
         col += count * LANES
     return plan
 
 
-def plan_scratch(plans):
-    return [shape for plan in plans for _, rows, _, width, by_cols in plan for shape in TorusSum.scratch(rows, width, by_cols)]
+def plan_scratch(plans, in_vmem=False):
+    return [shape for plan in plans for _, rows, _, width, by_cols in plan for shape in TorusSum.scratch(rows, width, by_cols, in_vmem)]
 
 
 def plan_sums(grads, plans, refs, in_vmem=False):
@@ -189,8 +186,9 @@
     for grad, plan in zip(grads, plans):
         groups.append([])
         for order, rows, col, width, by_cols in plan:
-            groups[-1].append(TorusSum(grad, order, rows, col, width, refs[:TorusSum.COUNT], by_cols, in_vmem))
-            refs = refs[TorusSum.COUNT:]
+            count = len(TorusSum.scratch(rows, width, by_cols, in_vmem))
+            groups[-1].append(TorusSum(grad, order, rows, col, width, refs[:count], by_cols, in_vmem))
+            refs = refs[count:]
     return groups
 
 
@@ -200,10 +198,14 @@
 PLAN_OUT = plan_columns(8, (4, 2, 2), True)
 
 
+def lane_mean(x):
+    return jnp.mean(x, axis=-1, keepdims=True)
+
+
 def normed(x):
     x = x.astype(F32)
-    centered = x - jnp.mean(x, axis=-1, keepdims=True)
-    rstd = lax.rsqrt(jnp.mean(centered * centered, axis=-1, keepdims=True) + NORM_EPS)
+    centered = x - lane_mean(x)
+    rstd = lax.rsqrt(lane_mean(centered * centered) + NORM_EPS)
     return centered * rstd, rstd
 
 
@@ -212,9 +214,9 @@
     return jnp.where(step < halves, core * halves + step, (1 - core) * halves + step - halves)
 
 
-def token_kernel(x_hbm, dy_hbm, ln_ref, freq_ref, wqkv_hbm, wout_hbm, wup_hbm, wdown_hbm,
-                 ha_ref, qkv_ref, dctx_ref, dhm_ref, cos_ref, sin_ref, dy_ref, gup_ref, gdown_ref,
-                 xs, dys, wqkv, wout, wup, wdown, ha_s, hm_s, hm_t, dh_s, up_acc, down_acc,
+def token_kernel(x_hbm, dy_hbm, ln_ref, freq_ref, wout_hbm, wup_hbm, wdown_hbm,
+                 ha_ref, dctx_ref, dh_ref, cos_ref, sin_ref, dy_ref, gup_ref, gdown_ref,
+                 xs, dys, wout, wup, wdown, ha_s, hm_s, hm_t, up_acc, down_acc,
                  row_load, w_load, chunk_load, flush_sem, dy_sem, send, recv):
     step = pl.program_id(0)
     first, last = step == 0, step == pl.num_programs(0) - 1
@@ -240,7 +242,7 @@
     core = lax.axis_index('tp')
     dy_saves = [pltpu.make_async_copy(dys.at[pl.ds(n * HALF, HALF)], dy_ref.at[pl.ds(place * HALF, HALF)], dy_sem.at[n])
                 for n, place in enumerate((core, 1 - core))]
-    w_loads = [pltpu.make_async_copy(src, dst, w_load.at[k]) for k, (src, dst) in enumerate(((wqkv_hbm, wqkv), (wout_hbm, wout)))]
+    w_loads = [pltpu.make_async_copy(wout_hbm, wout, w_load.at[0])]
     swaps = [send_to(other_core(), src, dst.at[pl.ds(HALF, HALF)], send.at[k], recv.at[k]) for k, (src, dst) in enumerate(((x_hbm, xs), (dy_hbm, dys)))]
 
     @pl.when(first)
@@ -253,36 +255,52 @@
         for copy in swaps:
             copy.start()
 
-    def norms(n):
-        norm, _ = normed(xs[pl.ds(pl.multiple_of(n * TT, TT), TT), :])
+    def norms(n, part):
+        size = TT // chunks
+        at = pl.ds(pl.multiple_of(part * size, size), size)
+        norm, _ = normed(xs[pl.ds(pl.multiple_of(n * TT + part * size, size), size), :])
         hm = (norm * ln_ref[pl.ds(2, 1), :] + ln_ref[pl.ds(3, 1), :]).astype(BF16)
-        ha_s[:] = (norm * ln_ref[pl.ds(0, 1), :] + ln_ref[pl.ds(1, 1), :]).astype(BF16).T
-        hm_s[:] = hm
-        hm_t[:] = hm.T
+        ha_s[:, at] = (norm * ln_ref[pl.ds(0, 1), :] + ln_ref[pl.ds(1, 1), :]).astype(BF16).T
+        slot = lax.rem(n, 2)
+        hm_s[slot, at, :] = hm
+        hm_t[slot, :, at] = hm.T
 
     @pl.when(first)
     def _():
         for copy in row_loads(0):
             copy.wait()
-        norms(0)
+        for part in range(chunks):
+            norms(0, part)
+        for n in range(1, HALF // TT):
+            for copy in row_loads(n):
+                copy.wait()
+
+    @pl.when(step == HALF // TT - 1)
+    def _():
+        for copy in swaps:
+            copy.wait_recv()
+        for copy in dy_saves:
+            copy.start()
 
     ha_ref[:] = ha_s[:]
+    now = lax.rem(step, 2)
 
     def columns(c, carry):
         @pl.when(first)
         def _():
             for copy in chunk_loads(c):
                 copy.wait()
+        norms(jnp.minimum(step + 1, pl.num_programs(0) - 1), c)
         cols = chunk(c)
-        u = dot(hm_s[:], wup[:, cols]).astype(BF16).astype(F32)
+        u = dot(hm_s[now], wup[:, cols]).astype(BF16).astype(F32)
         dg = dot_nt(dys[rows, :], wdown[cols, :]).astype(BF16).astype(F32)
         cdf = 0.5 * (1.0 + lax.erf(u * math.sqrt(0.5)))
         gelu = (u * cdf).astype(BF16)
         pdf = jnp.exp(-0.5 * u * u) * (1.0 / math.sqrt(2.0 * math.pi))
         dh = (dg * (cdf + u * pdf)).astype(BF16)
-        dh_s[:, cols] = dh
+        dh_ref[:, cols] = dh
         down_acc[cols, :] += dot(gelu.T, dys[rows, :])
-        up_acc[:, cols] += dot(hm_t[:], dh)
+        up_acc[:, cols] += dot(hm_t[now], dh)
 
         @pl.when(last)
         def _():
@@ -294,22 +312,6 @@
     def _():
         for copy in w_loads:
             copy.wait()
-    for n in range(1, HALF // TT):
-        @pl.when(step == n - 1)
-        def _(n=n):
-            for copy in row_loads(n):
-                copy.wait()
-
-    @pl.when(step == HALF // TT - 1)
-    def _():
-        for copy in swaps:
-            copy.wait_recv()
-        for copy in dy_saves:
-            copy.start()
-
-    dhm_ref[:] = dot_nt(dh_s[:], wup[:]).astype(BF16)
-    norms(jnp.minimum(step + 1, pl.num_programs(0) - 1))
-    qkv_ref[:] = dot(wqkv[:], ha_ref[:]).astype(BF16)
     dctx_ref[:] = dot_nt(wout[:], dys[rows, :]).astype(BF16)
     position = token_tile(step) * TT + lax.broadcasted_iota(jnp.int32, cos_ref.shape, 1)
     angles = position.astype(F32) * freq_ref[:, pl.ds(0, 1)]
@@ -327,7 +329,7 @@
                 copy.wait()
 
 
-def token_part(x, dy, ln, wqkv_t, wout, wup, wdown):
+def token_part(x, dy, ln, wout, wup, wdown):
     D, width = wup.shape
     S, V, dma = jax.ShapeDtypeStruct, pltpu.VMEM, pltpu.SemaphoreType.DMA
     hbm, vmem = pl.BlockSpec(memory_space=pl.ANY), pl.BlockSpec(memory_space=pltpu.VMEM)
@@ -343,22 +345,21 @@
     return pl.pallas_call(
         token_kernel,
         grid=(steps,),
-        in_specs=[hbm, hbm, vmem, vmem] + [hbm] * 4,
-        out_specs=[col(D), col(wqkv_t.shape[0]), col(wout.shape[0]), tok(D), col(HEAD // 2), col(HEAD // 2), hbm, hbm, hbm],
-        out_shape=[S((D, T), BF16), S((wqkv_t.shape[0], T), BF16), S((wout.shape[0], T), BF16), S((T, D), BF16),
+        in_specs=[hbm, hbm, vmem, vmem] + [hbm] * 3,
+        out_specs=[col(D), col(wout.shape[0]), tok(width), col(HEAD // 2), col(HEAD // 2), hbm, hbm, hbm],
+        out_shape=[S((D, T), BF16), S((wout.shape[0], T), BF16), S((T, width), BF16),
                    S((HEAD // 2, T), F32), S((HEAD // 2, T), F32), S((T, D), BF16),
                    S((D, width), F32), S((width, D), F32)],
-        scratch_shapes=[V((T, D), BF16)] * 2 + [V(w.shape, BF16) for w in (wqkv_t, wout, wup, wdown)]
-        + [V((D, TT), BF16), V((TT, D), BF16), V((D, TT), BF16), V((TT, width), BF16), V((D, width), F32), V((width, D), F32)]
-        + [dma((2, halves)), dma((2,)), dma((2, width // FC)), dma((2, width // FC)), dma((2,)), dma((2,)), dma((2,))],
+        scratch_shapes=[V((T, D), BF16)] * 2 + [V(w.shape, BF16) for w in (wout, wup, wdown)]
+        + [V((D, TT), BF16), V((2, TT, D), BF16), V((2, D, TT), BF16), V((D, width), F32), V((width, D), F32)]
+        + [dma((2, halves)), dma((1,)), dma((2, width // FC)), dma((2, width // FC)), dma((2,)), dma((2,)), dma((2,))],
         compiler_params=pltpu.CompilerParams(dimension_semantics=("arbitrary",), vmem_limit_bytes=VMEM_LIMIT,
                                              collective_id=2, has_side_effects=True),
-        cost_estimate=pl.CostEstimate(flops=52 * 10**9, bytes_accessed=60 << 20, transcendentals=2 * T * width),
         name="token_part",
-    )(x, dy, ln, freq, wqkv_t, wout, wup, wdown)
-
-
-def attention_pair(qkv_ref, dctx_ref, cos_ref, sin_ref, dqkv_ref, ctx_ref, q_t, k_t, q_n, k_n, v_n, do_n, p_s, dp_s, dk_acc, dv_acc, slot):
+    )(x, dy, ln, freq, wout, wup, wdown)
+
+
+def attention_pair(ha_ref, w_ref, dctx_ref, cos_ref, sin_ref, dqkv_ref, ctx_ref, qkv_ref, q_t, k_t, k_n, v_n, do_n, p_s, dp_s, dk_acc, dv_acc, slot):
     lane = lax.broadcasted_iota(jnp.int32, (TILE, PAIR), 1)
     key = lax.broadcasted_iota(jnp.int32, (TILE, 2 * TILE), 0)
     query = lax.broadcasted_iota(jnp.int32, (TILE, 2 * TILE), 1) % TILE
@@ -379,11 +380,11 @@
 
     def prepare(j):
         cols = tile_at(j)
+        qkv_ref[:, cols] = dot(w_ref[:], ha_ref[:, cols]).astype(BF16)
         for head in range(2):
             rows = pl.ds(head * HEAD, HEAD)
             q_t[rows, cols] = rotate(qkv_ref[head_rows(head, 0), cols], cols, 1.0) * jnp.asarray(HEAD ** -0.5, BF16)
             k_t[rows, cols] = rotate(qkv_ref[head_rows(head, 1), cols], cols, 1.0)
-        q_n[cols, :] = q_t[:, cols].T
         k_n[cols, :] = k_t[:, cols].T
         v_n[cols, :] = jnp.concatenate([qkv_ref[head_rows(head, 2), cols] for head in range(2)], axis=0).T
         do_n[cols, :] = dctx_ref[:, cols].T
@@ -444,7 +445,7 @@
 
     def grads(i, state):
         cols = tile_at(i)
-        q_pair, do_pair = split_lanes(q_n[cols, :]), split_lanes(do_n[cols, :])
+        do_pair = split_lanes(do_n[cols, :])
         ctx, dq = [None] * 2, [None] * 2
         for j in range(i + 1):
             keys = tile_at(j)
@@ -455,10 +456,14 @@
                 side = slice(head * TILE, (head + 1) * TILE)
                 ctx[head] = gather(ctx[head], dot(qkv_ref[head_rows(head, 2), keys], p_bf[:, side]), jnp.add)
                 dq[head] = gather(dq[head], dot(k_t[pl.ds(head * HEAD, HEAD), keys], ds_bf[:, side]), jnp.add)
-            for acc, new in ((dv_acc, dot(p_bf, do_pair)), (dk_acc, dot(ds_bf, q_pair))):
-                acc[keys, :] = new if i == blocks[0] else acc[keys, :] + new
+            dv = dot(p_bf, do_pair)
+            dv_acc[keys, :] = dv if i == blocks[0] else dv_acc[keys, :] + dv
+            for head in range(2):
+                rows = pl.ds(head * HEAD, HEAD)
+                dk = dot_nt(q_t[rows, cols], ds_bf[:, head * TILE:(head + 1) * TILE])
+                dk_acc[rows, keys] = dk if i == blocks[0] else dk_acc[rows, keys] + dk
             if j == i:
-                dk, dv = dk_acc[cols, :].astype(BF16).T, dv_acc[cols, :].astype(BF16).T
+                dk, dv = dk_acc[:, cols].astype(BF16), dv_acc[cols, :].astype(BF16).T
                 for head in range(2):
                     rows = pl.ds(head * HEAD, HEAD)
                     side = slice(head * HEAD, (head + 1) * HEAD)
@@ -485,20 +490,20 @@
             slot(SLOT_AFTER[n])
 
 
-P_TILES, DP_TILES = 21, 15
+P_TILES, DP_TILES = 16, 9
 SLOT_AFTER = {2: 1, 4: 2, 6: 3, 9: 4}
 
 
 def attention_scratch():
     V = pltpu.VMEM
-    return [V((PAIR, T), BF16)] * 2 + [V((T, PAIR), BF16)] * 4 + [V((P_TILES * TILE, 2 * TILE), F32), V((DP_TILES * TILE, 2 * TILE), BF16)] \
-        + [V((T, PAIR), F32)] * 2
+    return [V((3 * PAIR, T), BF16)] + [V((PAIR, T), BF16)] * 2 + [V((T, PAIR), BF16)] * 3 + [V((P_TILES * TILE, 2 * TILE), F32), V((DP_TILES * TILE, 2 * TILE), BF16)] \
+        + [V((PAIR, T), F32), V((T, PAIR), F32)]
 
 
 SCHEDULE = {
     (0, 0): (('start', 0),),
-    (1, 3): (('add', 0), ('pass_on', 0)),
-    (2, 3): (('finish', 0), ('start', 1)),
+    (1, 2): (('add', 0), ('pass_on', 0)),
+    (2, 2): (('finish', 0), ('start', 1)),
     (3, 1): (('add', 1), ('pass_on', 1)),
     (3, 2): (('finish', 1), ('start', 2)),
     (3, 3): (('add', 2), ('pass_on', 2)),
@@ -506,7 +511,7 @@
 }
 
 
-def attention_kernel(qkv_ref, dctx_ref, cos_ref, sin_ref, up_ref, down_ref, dqkv_ref, ctx_ref, up_out, down_out, *refs):
+def attention_kernel(ha_ref, w_ref, dctx_ref, cos_ref, sin_ref, up_ref, down_ref, dqkv_ref, ctx_ref, up_out, down_out, *refs):
     count = len(attention_scratch())
     groups = plan_sums((up_ref, down_ref), (PLAN_UP, PLAN_DOWN), refs[count:])
     every = groups[0] + groups[1]
@@ -529,10 +534,10 @@
                             out[:, one.cols] = one.result[:]
                             one.drain()
 
-    attention_pair(qkv_ref, dctx_ref, cos_ref, sin_ref, dqkv_ref, ctx_ref, *refs[:count], slot)
-
-
-def attention(qkv_t, dctx_t, cos_t, sin_t, g_up, g_down):
+    attention_pair(ha_ref, w_ref, dctx_ref, cos_ref, sin_ref, dqkv_ref, ctx_ref, *refs[:count], slot)
+
+
+def attention(ha_t, wqkv_t, dctx_t, cos_t, sin_t, g_up, g_down):
     pairs = dctx_t.shape[0] // PAIR
     S = jax.ShapeDtypeStruct
     shares = [(g.shape[0] // 64, g.shape[1]) for g in (g_up, g_down)]
@@ -547,31 +552,31 @@
     return pl.pallas_call(
         attention_kernel,
         grid=(pairs,),
-        in_specs=[by_pair(3 * PAIR), by_pair(PAIR), fixed(cos_t.shape), fixed(sin_t.shape), hbm, hbm],
+        in_specs=[fixed(ha_t.shape), pl.BlockSpec((3 * PAIR, wqkv_t.shape[1]), lambda p: (p, 0)), by_pair(PAIR), fixed(cos_t.shape), fixed(sin_t.shape), hbm, hbm],
         out_specs=[by_pair(3 * PAIR), by_pair(PAIR)] + [fixed(share) for share in shares],
-        out_shape=[S(qkv_t.shape, BF16), S(dctx_t.shape, BF16)] + [S(share, F32) for share in shares],
+        out_shape=[S((wqkv_t.shape[0], T), BF16), S(dctx_t.shape, BF16)] + [S(share, F32) for share in shares],
         scratch_shapes=attention_scratch() + plan_scratch((PLAN_UP, PLAN_DOWN)),
         compiler_params=pltpu.CompilerParams(dimension_semantics=("arbitrary",), vmem_limit_bytes=VMEM_LIMIT,
                                              collective_id=0, has_side_effects=True),
-        cost_estimate=pl.CostEstimate(flops=80 * 10**9, bytes_accessed=20 << 20, transcendentals=8 * T * T // 2),
         name="attention",
-    )(qkv_t, dctx_t, cos_t, sin_t, *(g.reshape((RING,) * 3 + (-1, g.shape[1])) for g in (g_up, g_down)))
-
-
-DURING_TOKENS = {2: ('B+0', 'b!0'), 5: ('C+0', 'c!0')}
-DURING_NORMS = {2: ('A=0',), 5: ('B=0', 'a+0'), 7: ('b+0',)}
+    )(ha_t, wqkv_t, dctx_t, cos_t, sin_t, *(g.reshape((RING,) * 3 + (-1, g.shape[1])) for g in (g_up, g_down)))
+
+
+DURING_TOKENS = {4: ('B+0', 'b!0')}
+DURING_MLP = {0: ('C+0', 'c!0'), 3: ('A=0', 'a+0')}
+DURING_NORMS = {0: ('B=0', 'b+0'), 2: ('C=0',), 4: ('c+0',), 5: ('A+1', 'a=0')}
 AFTER_NORMS = (
-    ('C=0', 'A+1', 'c+0', 'B+1', 'a=0', 'b=0'),
-    ('C+1', 'A=1', 'c=0', 'B=1', 'a+1', 'b+1'),
-    ('A+2', 'B+2', 'C=1', 'c+1', 'a=1', 'b=1'),
-    ('A=2', 'B=2', 'C+2', 'c=1', 'a+2', 'b+2'),
-    ('C=2', 'a=2', 'b=2', 'c+2', 'c=2'),
+    ('B+1', 'b=0', 'c=0', 'C+1', 'a+1', 'A=1'),
+    ('b+1', 'c+1', 'B=1', 'a=1', 'C=1', 'A+2'),
+    ('b=1', 'c=1', 'B+2', 'a+2', 'C+2', 'A=2'),
+    ('b+2', 'c+2', 'B=2', 'a=2', 'C=2'),
+    ('b=2', 'c=2'),
 )
 
 
-def tail_kernel(hat_hbm, dqkv_hbm, ctx_hbm, dy_hbm, w_hbm, x_hbm, dhm_hbm, ln_ref, gx_ref, gln_ref, gqkv_ref, gout_ref,
-                hat, dqkv, ctx, dy, w, x, dhm_own, dhm_in, dha_s, dha_in, g_qkv, g_out, pair_s, ring_s,
-                load, send, recv, ring_send, ring_recv, *sum_refs):
+def tail_kernel(hat_hbm, dqkv_hbm, ctx_hbm, dy_hbm, w_hbm, x_hbm, wup_hbm, dh_hbm, ln_ref, gx_ref, gln_ref, gqkv_ref, gout_ref,
+                hat, dqkv, ctx, dy, w, x, wup, dhm_s, dhm_in, dha_s, dha_in, g_qkv, g_out, pair_s, ring_s,
+                load, mlp_sem, send, recv, ring_send, ring_recv, *sum_refs):
     core = lax.axis_index('tp')
     own, away = core * HALF, (1 - core) * HALF
     groups = plan_sums((g_qkv, g_out), (PLAN_QKV, PLAN_OUT), sum_refs, True)
@@ -583,15 +588,14 @@
         return ref.at[pl.ds(start, size)]
 
     pieces = [(hat_hbm, hat)] + [(rows_of(dqkv_hbm, n * block, block), rows_of(dqkv, n * block, block)) for n in range(3)]
-    pieces += [(ctx_hbm, ctx), (dy_hbm, dy), (w_hbm, w), (x_hbm, x), (rows_of(dhm_hbm, own, HALF), dhm_own)]
+    pieces += [(ctx_hbm, ctx), (dy_hbm, dy), (w_hbm, w), (x_hbm, x), (wup_hbm, wup)]
     loads = [pltpu.make_async_copy(src, dst, load.at[n]) for n, (src, dst) in enumerate(pieces)]
     for copy in loads:
         copy.start()
     greet([ring_chip(axis, ahead) for axis in AXES for ahead in (1, 2, 3)] + [other_core()])
-    dhm_copy = send_to(other_core(), rows_of(dhm_hbm, away, HALF), dhm_in, send.at[0], recv.at[0])
+    dhm_copy = send_to(other_core(), dhm_s.at[0], dhm_in, send.at[0], recv.at[0])
     dha_copy = send_to(other_core(), dha_s.at[0], dha_in, send.at[1], recv.at[1])
     pair_copy = send_to(other_core(), pair_s.at[0], pair_s.at[1], send.at[2], recv.at[2])
-    dhm_copy.start()
 
     def run(events):
         for name, act, ring in events:
@@ -644,7 +648,13 @@
     lax.fori_loop(0, dy.shape[1] // TILE, out_columns, 0)
     run(('A+0', 'a!0'))
 
+    def mlp_load(k):
+        start = pl.multiple_of(jnp.where(k < 2, away, own) + lax.rem(k, 2) * TT, TT)
+        return pltpu.make_async_copy(rows_of(dh_hbm, start, TT), rows_of(hat, lax.rem(k, 2) * TT, TT), mlp_sem.at[lax.rem(k, 2)])
+
     loads[6].wait()
+    mlp_load(0).start()
+    mlp_load(1).start()
     tiles = HALF // TILE
 
     def tokens(k, carry):
@@ -660,8 +670,25 @@
         return carry
     lax.fori_loop(0, 2 * tiles, tokens, 0)
 
+    def mlp_tokens(k, carry):
+        run_at(k, DURING_MLP)
+        mlp_load(k).wait()
+        half, mine = lax.rem(k, 2) * TT, lax.div(k, 2)
+        at = pl.ds(pl.multiple_of(half, TT), TT)
+        dhm_s[mine, at, :] = dot_nt(hat[at, :], wup[:]).astype(BF16)
+
+        @pl.when(k < 2)
+        def _():
+            mlp_load(k + 2).start()
+
+        @pl.when(k == 1)
+        def _():
+            dhm_copy.start()
+        return carry
+    loads[8].wait()
+    lax.fori_loop(0, T // TT, mlp_tokens, 0)
+
     loads[7].wait()
-    loads[8].wait()
     dhm_copy.wait_recv()
     dha_copy.wait_recv()
     pair_s[0] = jnp.zeros_like(pair_s[0])
@@ -670,10 +697,10 @@
         at = pl.ds(pl.multiple_of(k * SMALL, SMALL), SMALL)
         norm, rstd = normed(x[at, :])
         da = (dha_s[1, at, :].astype(F32) + dha_in[at, :].astype(F32)).astype(BF16).astype(F32)
-        dm = (dhm_own[at, :].astype(F32) + dhm_in[at, :].astype(F32)).astype(BF16).astype(F32)
+        dm = (dhm_s[1, at, :].astype(F32) + dhm_in[at, :].astype(F32)).astype(BF16).astype(F32)
         g = da * ln_ref[pl.ds(0, 1), :] + dm * ln_ref[pl.ds(2, 1), :]
-        mean_g = jnp.mean(g, axis=-1, keepdims=True)
-        mean_gn = jnp.mean(g * norm, axis=-1, keepdims=True)
+        mean_g = lane_mean(g)
+        mean_gn = lane_mean(g * norm)
         residual = dy[pl.ds(pl.multiple_of(own + k * SMALL, SMALL), SMALL), :].astype(F32)
         gx_ref[at, :] = (residual + rstd * (g - mean_g - norm * mean_gn)).astype(BF16)
         for row, value in enumerate((da * norm, da, dm * norm, dm)):
@@ -720,7 +747,7 @@
             copy.wait_send()
 
 
-def tail(ha_t, dqkv_t, ctx_t, dy, wqkv_t, x, dhm, ln):
+def tail(ha_t, dqkv_t, ctx_t, dy, wqkv_t, x, wup, dh, ln):
     D, C = ha_t.shape[0], ctx_t.shape[0]
     S, V = jax.ShapeDtypeStruct, pltpu.VMEM
     hbm, vmem = pl.BlockSpec(memory_space=pl.ANY), pl.BlockSpec(memory_space=pltpu.VMEM)
@@ -729,16 +756,15 @@
     dma = pltpu.SemaphoreType.DMA
     return pl.pallas_call(
         tail_kernel,
-        in_specs=[hbm] * 7 + [vmem],
+        in_specs=[hbm] * 8 + [vmem],
         out_specs=[vmem] * 4,
         out_shape=[S((HALF, D), BF16), S(ln.shape, F32), S((D // 64, 3, C // HEAD, HEAD), F32), S((C // 64, D), F32)],
-        scratch_shapes=[V(a.shape, BF16) for a in (ha_t, dqkv_t, ctx_t, dy, wqkv_t)] + [own] * 3 + [V((2, HALF, D), BF16), own]
+        scratch_shapes=[V(a.shape, BF16) for a in (ha_t, dqkv_t, ctx_t, dy, wqkv_t, x, wup)] + [V((2, HALF, D), BF16), own] * 2
         + [V(chips + (D // 64, 3 * C), F32), V(chips + (C // 64, D), F32), V((2, 8, D), F32), V((3, RING, 8, D), F32)]
-        + [dma((9,)), dma((3,)), dma((3,)), dma((3, RING)), dma((3, RING))] + plan_scratch((PLAN_QKV, PLAN_OUT)),
+        + [dma((9,)), dma((2,)), dma((3,)), dma((3,)), dma((3, RING)), dma((3, RING))] + plan_scratch((PLAN_QKV, PLAN_OUT), True),
         compiler_params=pltpu.CompilerParams(vmem_limit_bytes=VMEM_LIMIT, collective_id=1, has_side_effects=True),
-        cost_estimate=pl.CostEstimate(flops=15 * 10**9, bytes_accessed=30 << 20, transcendentals=0),
         name="tail",
-    )(ha_t, dqkv_t, ctx_t, dy, wqkv_t, x, dhm, ln)
+    )(ha_t, dqkv_t, ctx_t, dy, wqkv_t, x, wup, dh, ln)
 
 
 def output_kernel(*refs):
@@ -770,9 +796,9 @@
     def local_step(x_loc, dy_loc, ln_params, w_qkv, w_out, w_up, w_down):
         x_loc, dy_loc = x_loc[0], dy_loc[0]
         wqkv_t = w_qkv.transpose(1, 2, 3, 0).reshape(-1, x_loc.shape[1])
-        ha_t, qkv_t, dctx_t, dhm, cos_t, sin_t, dy, g_wup, g_wdown = token_part(x_loc, dy_loc, ln_params, wqkv_t, w_out, w_up, w_down)
-        dqkv_t, ctx_t, grad_wup, grad_wdown = attention(qkv_t, dctx_t, cos_t, sin_t, g_wup, g_wdown)
-        grad_x, grad_ln, grad_wqkv, grad_wout = tail(ha_t, dqkv_t, ctx_t, dy, wqkv_t, x_loc, dhm, ln_params)
+        ha_t, dctx_t, dh, cos_t, sin_t, dy, g_wup, g_wdown = token_part(x_loc, dy_loc, ln_params, w_out, w_up, w_down)
+        dqkv_t, ctx_t, grad_wup, grad_wdown = attention(ha_t, wqkv_t, dctx_t, cos_t, sin_t, g_wup, g_wdown)
+        grad_x, grad_ln, grad_wqkv, grad_wout = tail(ha_t, dqkv_t, ctx_t, dy, wqkv_t, x_loc, w_up, dh, ln_params)
         grad_x, grad_ln, grad_wqkv, *rest = outputs(grad_x, grad_ln, grad_wqkv, grad_wout, grad_wup, grad_wdown)
         return grad_x[None], grad_ln, grad_wqkv.swapaxes(1, 2), *rest
 

time: 214 us -> 207 us (0.967)
  Pallas kernels: 213 us -> 206 us
    pallas_call x1, Pallas kernels: 67 us -> 56 us  [token_part(): pl.pallas_call(token_kernel, grid=(steps,), in_specs=[hbm, hbm, vmem, vme...]
    pallas_call x2, Pallas kernels: 143 us -> 147 us  [the longest x1 88.1 us: attention(): pl.pallas_call(attention_kernel, grid=(pairs,), in_specs=[fixed(ha_t.shap...]
where the time goes in v2:
time: 207 us; the launch traced here: 206 us
  Pallas kernels  206 us (100%)
    pallas_call x1, Pallas kernels, attention(): pl.pallas_call(attention_kernel, grid=(pairs,), in_specs=[fixed(ha_t.shap...  88.1 us
    pallas_call x1, Pallas kernels, tail(): pl.pallas_call(tail_kernel, in_specs=[hbm] * 8 + [vmem], out_specs=[vmem]...  58.5 us
    pallas_call x1, Pallas kernels, token_part(): pl.pallas_call(token_kernel, grid=(steps,), in_specs=[hbm, hbm, vmem, vme...  56 us

profile of v2, /device:TPU:0, one launch (start us, length us, event | category | flops | bytes accessed | tf_op | source)
XLA Modules:
  0.0 206.4 jit_solution(16752909949095914784)
XLA Ops:
  0.6 56.0 %token_part.1 = (bf16[1024,2048]{1,0:T(8,128)(2,1)}, bf16[512,2048]{1,0:T(8,128)(2,1)}, bf16[2048,2048]{1,0:T(8,128)(2,1)}, f32[32,2048]{1,0:T(8,128)}, f32[32,2...) custom-call(bf16[1024,1024]{1,0:T(8,128)(2,1)} %bitcast.13, ...), custom_call_target="tpu_custom_call" | custom-call | tf_op jit(solution)/shard_map/token_part/pallas_call | solution.py:345
  56.7 88.1 %attention.1 = (bf16[1536,2048]{1,0:T(8,128)(2,1)}, bf16[512,2048]{1,0:T(8,128)(2,1)}, f32[16,2048]{1,0:T(8,128)}, f32[32,1024]{1,0:T(8,128)}) custom-call(bf16[1024,2048]{1,0:T(8,128)(2,1)} %get-tuple-element.28.ha_ref.hat_hbm, bf16[1536,1024]{1,0:T(8,128)(2,1)} %bitcast.9, bf16[512,2048]{1,0:T(8,128)(2,1)} %get-tuple-element.29.dctx_ref, ...), custom_call_target="tpu_custom_call" | custom-call | tf_op jit(solution)/shard_map/attention/pallas_call | solution.py:552
  144.8 58.5 %tail.1 = (bf16[1024,1024]{1,0:T(8,128)(2,1)}, f32[4,1024]{1,0:T(4,128)}, f32[16,3,8,64]{3,2,1,0:T(8,128)}, f32[8,1024]{1,0:T(8,128)}) custom-call(bf16[1024,2048]{1,0:T(8,128)(2,1)} %get-tuple-element.28.ha_ref.hat_hbm, bf16[1536,2048]{1,0:T(8,128)(2,1)} %get-tuple-element.34.dqkv_hbm, bf16[512,2048]{1,0:T(8,128)(2,1)} %get-tuple-element.35.ctx_hbm, ...), custom_call_target="tpu_custom_call" | custom-call | tf_op jit(solution)/shard_map/tail/pallas_call | solution.py:757
  203.3 2.9 %outputs.1 = (bf16[1024,1024]{1,0:T(8,128)(2,1)}, f32[4,1024]{1,0:T(4,128)}, f32[16,3,8,64]{3,2,1,0:T(8,128)}, f32[8,1024]{1,0:T(8,128)}, f32[16,2048]{1,0:T(8,128)}, /*index=5*/f32[32,1024]{1,0:T(8,128)}) custom-call(bf16[1024,1024]{1,0:T(8,128)(2,1)} %get-tuple-element.38.refs_0_, f32[4,1024]{1,0:T(4,128)} %get-tuple-element.39.refs_1_, ...), custom_call_target="tpu_custom_call" | custom-call | tf_op jit(solution)/shard_map/outputs/pallas_call | solution.py:787

commit v3 on v2

--- a/solution.py
+++ b/solution.py
@@ -15,7 +15,7 @@
 T = 2048
 HALF = T // 2
 TILE = 256
-SMALL = 128
+SMALL = 256
 TT = 512
 FC = 1024
 LANES = 128
@@ -32,6 +32,10 @@
 
 def dot_nt(a, b):
     return lax.dot_general(a, b, (((1,), (1,)), ((), ())), preferred_element_type=F32)
+
+
+def row_of(ref, n):
+    return ref[pl.ds(n, 1), :]
 
 
 def ring_place(axis):
@@ -259,8 +263,8 @@
         size = TT // chunks
         at = pl.ds(pl.multiple_of(part * size, size), size)
         norm, _ = normed(xs[pl.ds(pl.multiple_of(n * TT + part * size, size), size), :])
-        hm = (norm * ln_ref[pl.ds(2, 1), :] + ln_ref[pl.ds(3, 1), :]).astype(BF16)
-        ha_s[:, at] = (norm * ln_ref[pl.ds(0, 1), :] + ln_ref[pl.ds(1, 1), :]).astype(BF16).T
+        hm = (norm * row_of(ln_ref, 2) + row_of(ln_ref, 3)).astype(BF16)
+        ha_s[:, at] = (norm * row_of(ln_ref, 0) + row_of(ln_ref, 1)).astype(BF16).T
         slot = lax.rem(n, 2)
         hm_s[slot, at, :] = hm
         hm_t[slot, :, at] = hm.T
@@ -502,8 +506,8 @@
 
 SCHEDULE = {
     (0, 0): (('start', 0),),
-    (1, 2): (('add', 0), ('pass_on', 0)),
-    (2, 2): (('finish', 0), ('start', 1)),
+    (1, 3): (('add', 0), ('pass_on', 0)),
+    (2, 3): (('finish', 0), ('start', 1)),
     (3, 1): (('add', 1), ('pass_on', 1)),
     (3, 2): (('finish', 1), ('start', 2)),
     (3, 3): (('add', 2), ('pass_on', 2)),
@@ -562,20 +566,20 @@
     )(ha_t, wqkv_t, dctx_t, cos_t, sin_t, *(g.reshape((RING,) * 3 + (-1, g.shape[1])) for g in (g_up, g_down)))
 
 
-DURING_TOKENS = {4: ('B+0', 'b!0')}
-DURING_MLP = {0: ('C+0', 'c!0'), 3: ('A=0', 'a+0')}
-DURING_NORMS = {0: ('B=0', 'b+0'), 2: ('C=0',), 4: ('c+0',), 5: ('A+1', 'a=0')}
+DURING_TOKENS = {2: ('B+0', 'b!0'), 5: ('C+0', 'c!0')}
+DURING_MLP = {2: ('A=0', 'a+0'), 3: ('B=0', 'b+0')}
+DURING_NORMS = {0: ('C=0', 'c+0'), 1: ('A+1', 'a=0'), 2: ('B+1', 'b=0'), 3: ('c=0', 'C+1')}
 AFTER_NORMS = (
-    ('B+1', 'b=0', 'c=0', 'C+1', 'a+1', 'A=1'),
-    ('b+1', 'c+1', 'B=1', 'a=1', 'C=1', 'A+2'),
-    ('b=1', 'c=1', 'B+2', 'a+2', 'C+2', 'A=2'),
-    ('b+2', 'c+2', 'B=2', 'a=2', 'C=2'),
-    ('b=2', 'c=2'),
+    ('a+1', 'A=1', 'B=1', 'b+1'),
+    ('c+1', 'C=1', 'A+2', 'a=1', 'B+2', 'b=1'),
+    ('c=1', 'C+2', 'A=2', 'a+2', 'b+2', 'B=2'),
+    ('c+2', 'a=2', 'b=2', 'C=2'),
+    ('c=2',),
 )
 
 
 def tail_kernel(hat_hbm, dqkv_hbm, ctx_hbm, dy_hbm, w_hbm, x_hbm, wup_hbm, dh_hbm, ln_ref, gx_ref, gln_ref, gqkv_ref, gout_ref,
-                hat, dqkv, ctx, dy, w, x, wup, dhm_s, dhm_in, dha_s, dha_in, g_qkv, g_out, pair_s, ring_s,
+                gx_s, hat, dqkv, ctx, dy, w, x, wup, dhm_s, dhm_in, dha_s, dha_in, g_qkv, g_out, pair_s, ring_s,
                 load, mlp_sem, send, recv, ring_send, ring_recv, *sum_refs):
     core = lax.axis_index('tp')
     own, away = core * HALF, (1 - core) * HALF
@@ -692,19 +696,22 @@
     dhm_copy.wait_recv()
     dha_copy.wait_recv()
     pair_s[0] = jnp.zeros_like(pair_s[0])
+    wide = pair_s.shape[2]
 
     def norm_back(k, carry):
         at = pl.ds(pl.multiple_of(k * SMALL, SMALL), SMALL)
         norm, rstd = normed(x[at, :])
         da = (dha_s[1, at, :].astype(F32) + dha_in[at, :].astype(F32)).astype(BF16).astype(F32)
         dm = (dhm_s[1, at, :].astype(F32) + dhm_in[at, :].astype(F32)).astype(BF16).astype(F32)
-        g = da * ln_ref[pl.ds(0, 1), :] + dm * ln_ref[pl.ds(2, 1), :]
+        g = da * row_of(ln_ref, 0) + dm * row_of(ln_ref, 2)
         mean_g = lane_mean(g)
         mean_gn = lane_mean(g * norm)
         residual = dy[pl.ds(pl.multiple_of(own + k * SMALL, SMALL), SMALL), :].astype(F32)
-        gx_ref[at, :] = (residual + rstd * (g - mean_g - norm * mean_gn)).astype(BF16)
+        gx_s[at, :] = (residual + rstd * (g - mean_g - norm * mean_gn)).astype(BF16)
         for row, value in enumerate((da * norm, da, dm * norm, dm)):
-            pair_s[0, pl.ds(row, 1), :] += jnp.sum(value, axis=0, keepdims=True)
+            total = jnp.sum(value, axis=0, keepdims=True)
+            for side in range(2):
+                pair_s[0, pl.ds(2 * row + side, 1), :] += total[:, side * wide:(side + 1) * wide]
         return carry
 
     steps = HALF // SMALL
@@ -714,6 +721,8 @@
         return norm_back(k, carry)
     lax.fori_loop(0, steps, norm_step, 0)
     pair_copy.start()
+    gx_copy = pltpu.make_async_copy(gx_s, gx_ref, load.at[9])
+    gx_copy.start()
 
     def ring_copies(phase):
         place = ring_place(AXES[phase])
@@ -737,10 +746,15 @@
             ring_start(0, pair_s[0] + pair_s[1])
         elif n < len(AXES):
             ring_start(n, ring_sum(n - 1))
-    gln_ref[:] = ring_sum(2)[:gln_ref.shape[0]]
+    pair_copy.wait_send()
+    pair_s[0] = ring_sum(2)
+    for row in range(gln_ref.shape[0]):
+        for side in range(2):
+            gln_ref[pl.ds(row, 1), pl.ds(side * wide, wide)] = row_of(pair_s.at[0], 2 * row + side)
     for one in sums.values():
         one.drain()
-    for copy in (dhm_copy, dha_copy, pair_copy):
+    gx_copy.wait()
+    for copy in (dhm_copy, dha_copy):
         copy.wait_send()
     for phase in range(3):
         for copy in ring_copies(phase):
@@ -757,11 +771,11 @@
     return pl.pallas_call(
         tail_kernel,
         in_specs=[hbm] * 8 + [vmem],
-        out_specs=[vmem] * 4,
+        out_specs=[hbm] + [vmem] * 3,
         out_shape=[S((HALF, D), BF16), S(ln.shape, F32), S((D // 64, 3, C // HEAD, HEAD), F32), S((C // 64, D), F32)],
-        scratch_shapes=[V(a.shape, BF16) for a in (ha_t, dqkv_t, ctx_t, dy, wqkv_t, x, wup)] + [V((2, HALF, D), BF16), own] * 2
-        + [V(chips + (D // 64, 3 * C), F32), V(chips + (C // 64, D), F32), V((2, 8, D), F32), V((3, RING, 8, D), F32)]
-        + [dma((9,)), dma((2,)), dma((3,)), dma((3,)), dma((3, RING)), dma((3, RING))] + plan_scratch((PLAN_QKV, PLAN_OUT), True),
+        scratch_shapes=[own] + [V(a.shape, BF16) for a in (ha_t, dqkv_t, ctx_t, dy, wqkv_t, x, wup)] + [V((2, HALF, D), BF16), own] * 2
+        + [V(chips + (D // 64, 3 * C), F32), V(chips + (C // 64, D), F32), V((2, 8, D // 2), F32), V((3, RING, 8, D // 2), F32)]
+        + [dma((10,)), dma((2,)), dma((3,)), dma((3,)), dma((3, RING)), dma((3, RING))] + plan_scratch((PLAN_QKV, PLAN_OUT), True),
         compiler_params=pltpu.CompilerParams(vmem_limit_bytes=VMEM_LIMIT, collective_id=1, has_side_effects=True),
         name="tail",
     )(ha_t, dqkv_t, ctx_t, dy, wqkv_t, x, wup, dh, ln)

time: 207 us -> 203 us (0.981)
  Pallas kernels: 206 us -> 202 us
    pallas_call x1, Pallas kernels: 58.5 us -> 55.6 us  [tail(): pl.pallas_call(tail_kernel, in_specs=[hbm] * 8 + [vmem], out_specs=[hbm]...]
where the time goes in v3:
time: 203 us; the launch traced here: 202 us
  Pallas kernels  202 us (100%)
    pallas_call x1, Pallas kernels, attention(): pl.pallas_call(attention_kernel, grid=(pairs,), in_specs=[fixed(ha_t.shap...  87 us
    pallas_call x1, Pallas kernels, token_part(): pl.pallas_call(token_kernel, grid=(steps,), in_specs=[hbm, hbm, vmem, vme...  56 us
    pallas_call x1, Pallas kernels, tail(): pl.pallas_call(tail_kernel, in_specs=[hbm] * 8 + [vmem], out_specs=[hbm]...  55.6 us

profile of v3, /device:TPU:0, one launch (start us, length us, event | category | flops | bytes accessed | tf_op | source)
XLA Modules:
  0.0 202.4 jit_solution(1053789952886509195)
XLA Ops:
  0.6 56.0 %token_part.1 = (bf16[1024,2048]{1,0:T(8,128)(2,1)}, bf16[512,2048]{1,0:T(8,128)(2,1)}, bf16[2048,2048]{1,0:T(8,128)(2,1)}, f32[32,2048]{1,0:T(8,128)}, f32[32,2...) custom-call(bf16[1024,1024]{1,0:T(8,128)(2,1)} %bitcast.13, ...), custom_call_target="tpu_custom_call" | custom-call | tf_op jit(solution)/shard_map/token_part/pallas_call | solution.py:349
  56.7 87.0 %attention.1 = (bf16[1536,2048]{1,0:T(8,128)(2,1)}, bf16[512,2048]{1,0:T(8,128)(2,1)}, f32[16,2048]{1,0:T(8,128)}, f32[32,1024]{1,0:T(8,128)}) custom-call(bf16[1024,2048]{1,0:T(8,128)(2,1)} %get-tuple-element.28.ha_ref.hat_hbm, bf16[1536,1024]{1,0:T(8,128)(2,1)} %bitcast.9, bf16[512,2048]{1,0:T(8,128)(2,1)} %get-tuple-element.29.dctx_ref, ...), custom_call_target="tpu_custom_call" | custom-call | tf_op jit(solution)/shard_map/attention/pallas_call | solution.py:556
  143.7 55.6 %tail.1 = (bf16[1024,1024]{1,0:T(8,128)(2,1)}, f32[4,1024]{1,0:T(4,128)}, f32[16,3,8,64]{3,2,1,0:T(8,128)}, f32[8,1024]{1,0:T(8,128)}) custom-call(bf16[1024,2048]{1,0:T(8,128)(2,1)} %get-tuple-element.28.ha_ref.hat_hbm, bf16[1536,2048]{1,0:T(8,128)(2,1)} %get-tuple-element.34.dqkv_hbm, bf16[512,2048]{1,0:T(8,128)(2,1)} %get-tuple-element.35.ctx_hbm, ...), custom_call_target="tpu_custom_call" | custom-call | tf_op jit(solution)/shard_map/tail/pallas_call | solution.py:771
  199.3 2.9 %outputs.1 = (bf16[1024,1024]{1,0:T(8,128)(2,1)}, f32[4,1024]{1,0:T(4,128)}, f32[16,3,8,64]{3,2,1,0:T(8,128)}, f32[8,1024]{1,0:T(8,128)}, f32[16,2048]{1,0:T(8,128)}, /*index=5*/f32[32,1024]{1,0:T(8,128)}) custom-call(bf16[1024,1024]{1,0:T(8,128)(2,1)} %get-tuple-element.38.refs_0_, f32[4,1024]{1,0:T(4,128)} %get-tuple-element.39.refs_1_, ...), custom_call_target="tpu_custom_call" | custom-call | tf_op jit(solution)/shard_map/outputs/pallas_call | solution.py:801

commit v4 on v3

--- a/solution.py
+++ b/solution.py
@@ -294,7 +294,6 @@
         def _():
             for copy in chunk_loads(c):
                 copy.wait()
-        norms(jnp.minimum(step + 1, pl.num_programs(0) - 1), c)
         cols = chunk(c)
         u = dot(hm_s[now], wup[:, cols]).astype(BF16).astype(F32)
         dg = dot_nt(dys[rows, :], wdown[cols, :]).astype(BF16).astype(F32)
@@ -303,8 +302,9 @@
         pdf = jnp.exp(-0.5 * u * u) * (1.0 / math.sqrt(2.0 * math.pi))
         dh = (dg * (cdf + u * pdf)).astype(BF16)
         dh_ref[:, cols] = dh
+        up_acc[:, cols] += dot(hm_t[now], dh)
         down_acc[cols, :] += dot(gelu.T, dys[rows, :])
-        up_acc[:, cols] += dot(hm_t[now], dh)
+        norms(jnp.minimum(step + 1, pl.num_programs(0) - 1), c)
 
         @pl.when(last)
         def _():

time: 203 us -> 199 us (0.980)
  Pallas kernels: 202 us -> 198 us
    pallas_call x1, Pallas kernels: 56 us -> 52.6 us  [token_part(): pl.pallas_call(token_kernel, grid=(steps,), in_specs=[hbm, hbm, vmem, vme...]
where the time goes in v4:
time: 199 us
  Pallas kernels  198 us (99%)
    pallas_call x1, Pallas kernels, attention(): pl.pallas_call(attention_kernel, grid=(pairs,), in_specs=[fixed(ha_t.shap...  87 us
    pallas_call x1, Pallas kernels, tail(): pl.pallas_call(tail_kernel, in_specs=[hbm] * 8 + [vmem], out_specs=[hbm]...  55.6 us
    pallas_call x1, Pallas kernels, token_part(): pl.pallas_call(token_kernel, grid=(steps,), in_specs=[hbm, hbm, vmem, vme...  52.6 us

profile of v4, /device:TPU:0, one launch (start us, length us, event | category | flops | bytes accessed | tf_op | source)
XLA Modules:
  0.0 198.9 jit_solution(6438650222564979468)
XLA Ops:
  0.6 52.6 %token_part.1 = (bf16[1024,2048]{1,0:T(8,128)(2,1)}, bf16[512,2048]{1,0:T(8,128)(2,1)}, bf16[2048,2048]{1,0:T(8,128)(2,1)}, f32[32,2048]{1,0:T(8,128)}, f32[32,2...) custom-call(bf16[1024,1024]{1,0:T(8,128)(2,1)} %bitcast.13, ...), custom_call_target="tpu_custom_call" | custom-call | tf_op jit(solution)/shard_map/token_part/pallas_call | solution.py:349
  53.2 87.0 %attention.1 = (bf16[1536,2048]{1,0:T(8,128)(2,1)}, bf16[512,2048]{1,0:T(8,128)(2,1)}, f32[16,2048]{1,0:T(8,128)}, f32[32,1024]{1,0:T(8,128)}) custom-call(bf16[1024,2048]{1,0:T(8,128)(2,1)} %get-tuple-element.28.ha_ref.hat_hbm, bf16[1536,1024]{1,0:T(8,128)(2,1)} %bitcast.9, bf16[512,2048]{1,0:T(8,128)(2,1)} %get-tuple-element.29.dctx_ref, ...), custom_call_target="tpu_custom_call" | custom-call | tf_op jit(solution)/shard_map/attention/pallas_call | solution.py:556
  140.2 55.6 %tail.1 = (bf16[1024,1024]{1,0:T(8,128)(2,1)}, f32[4,1024]{1,0:T(4,128)}, f32[16,3,8,64]{3,2,1,0:T(8,128)}, f32[8,1024]{1,0:T(8,128)}) custom-call(bf16[1024,2048]{1,0:T(8,128)(2,1)} %get-tuple-element.28.ha_ref.hat_hbm, bf16[1536,2048]{1,0:T(8,128)(2,1)} %get-tuple-element.34.dqkv_hbm, bf16[512,2048]{1,0:T(8,128)(2,1)} %get-tuple-element.35.ctx_hbm, ...), custom_call_target="tpu_custom_call" | custom-call | tf_op jit(solution)/shard_map/tail/pallas_call | solution.py:771
  195.9 2.9 %outputs.1 = (bf16[1024,1024]{1,0:T(8,128)(2,1)}, f32[4,1024]{1,0:T(4,128)}, f32[16,3,8,64]{3,2,1,0:T(8,128)}, f32[8,1024]{1,0:T(8,128)}, f32[16,2048]{1,0:T(8,128)}, /*index=5*/f32[32,1024]{1,0:T(8,128)}) custom-call(bf16[1024,1024]{1,0:T(8,128)(2,1)} %get-tuple-element.38.refs_0_, f32[4,1024]{1,0:T(4,128)} %get-tuple-element.39.refs_1_, ...), custom_call_target="tpu_custom_call" | custom-call | tf_op jit(solution)/shard_map/outputs/pallas_call | solution.py:801
